TPU v7x, 32 devices: a whole 2x2x4 slice. The times are simulated.
32 devices in a mesh: gx: 4 (over y, x), gy: 8 (over z, core).
Axes of the slice: x: 2, y: 2, z: 4, core: 2. Of those that a mesh axis runs over, the one named last changes fastest.
Arguments:
- e_field: float32 [3, 128, 256, 128], P(None, 'gx', 'gy'), may hold values from -6 to 6
- h_field: float32 [3, 128, 256, 128], P(None, 'gx', 'gy'), may hold values from -6 to 6
- psi: float32 [12, 128, 256, 128], P(None, 'gx', 'gy'), may hold values from -6 to 6
- material: int32 [128, 256, 128], P('gx', 'gy'), may hold values from 0 to 7
- eps_table: float32 [8], replicated, may hold values from 1 to 1.2
- sigma_table: float32 [8], replicated, may hold values from 0 to 0.05
Outputs:
- e_out: float32 [3, 128, 256, 128], P(None, 'gx', 'gy')
- h_out: float32 [3, 128, 256, 128], P(None, 'gx', 'gy')
- psi_out: float32 [12, 128, 256, 128], P(None, 'gx', 'gy')
All inputs are finite; a program needn't handle non-finite values.
Results may differ from a plain program's by a relative error of at most 0.0003.
Values sent between devices are 32-bit elements; how exact they have to be, the bound alone decides.
A program may use at most 128 MiB of HBM per device.

v0:
```python
import jax
import jax.numpy as jnp
from jax import lax
from jax.experimental import pallas as pl
from jax.experimental.pallas import tpu as pltpu
from jax.sharding import PartitionSpec as P

PML = 16
STEPS = 16
NMAT = 8
SUB = 8
GROUP = 16
AHEAD = 2

time_step = 0.5
sigma_peak = 3.0
kappa_peak = 5.0
alpha_peak = 0.05
MESH = pl.DeviceIdType.MESH


def profile(index, extent, shift_half):
    position = index.astype(jnp.float32) + shift_half
    slab_width = float(PML)
    depth_frac = jnp.maximum(
        jnp.maximum(
            (slab_width - position) / slab_width, (position - (extent - slab_width)) / slab_width
        ),
        0.0,
    )
    depth_cube = depth_frac * depth_frac * depth_frac
    sigma_value = sigma_peak * depth_cube
    kappa_value = 1.0 + (kappa_peak - 1.0) * depth_cube
    alpha_value = alpha_peak * (1.0 - depth_frac)
    decays = jnp.exp(-(sigma_value / kappa_value + alpha_value) * time_step)
    scaling = (
        sigma_value * (decays - 1.0) / (kappa_value * (sigma_value + kappa_value * alpha_value))
    )
    inside_slab = depth_frac > 0.0
    return (
        jnp.where(inside_slab, decays, 0.0),
        jnp.where(inside_slab, scaling, 0.0),
        1.0 / kappa_value,
    )


def make_kernel(size_x, size_y, rows_x, rows_y, depth_z):
    groups = rows_x // GROUP
    tiles = rows_y // SUB
    top, right = rows_x - 1, rows_y - 1

    def kernel(
        e_in, h_in, p_in, m_in, eps_ref, sig_ref, E, H, S,
        keep, drive, mat, cx, cy,
        t_ex, t_ey, t_ax, t_ay, t_c0, t_c1,
        r_ex, r_ey, r_ax, r_ay, r_c0, r_c1,
        in_sem, send_sem, recv_sem,
    ):
        gx, gy = lax.axis_index("gx"), lax.axis_index("gy")
        has_lx, has_hx = gx > 0, gx < size_x - 1
        has_ly, has_hy = gy > 0, gy < size_y - 1
        slab_x = (gx == 0, gx == size_x - 1)
        slab_y = (gy == 0, gy == size_y - 1)
        lx, hx, ly, hy = gx - 1, gx + 1, gy - 1, gy + 1
        both = jnp.logical_and
        links = (
            (has_lx, (lx, gy)),
            (has_hx, (hx, gy)),
            (has_ly, (gx, ly)),
            (has_hy, (gx, hy)),
            (both(has_hx, has_ly), (hx, ly)),
            (both(has_lx, has_hy), (lx, hy)),
        )

        plain = [
            (e_in, E.at[:, pl.ds(0, rows_x), pl.ds(0, rows_y), :]),
            (h_in, H.at[:, pl.ds(1, rows_x), pl.ds(SUB, rows_y), :]),
            (m_in, mat),
            (p_in.at[pl.ds(1, 2)], S.at[pl.ds(1, 2)]),
            (p_in.at[pl.ds(7, 2)], S.at[pl.ds(7, 2)]),
        ]
        copies = [pltpu.make_async_copy(a, b, in_sem.at[n]) for n, (a, b) in enumerate(plain)]
        for c in copies:
            c.start()

        def slab_copies(side):
            half_x = pl.ds(side * PML, PML)
            xs = [
                pltpu.make_async_copy(
                    p_in.at[pl.ds(s, 2), half_x], S.at[pl.ds(s, 2), half_x], in_sem.at[5 + n]
                )
                for n, s in enumerate((3, 9))
            ]
            ys = [
                pltpu.make_async_copy(
                    p_in.at[s, :, half_x], S.at[s, :, half_x], in_sem.at[7 + n]
                )
                for n, s in enumerate((0, 5, 6, 11))
            ]
            return xs, ys

        for side in (0, 1):
            xs, ys = slab_copies(side)

            @pl.when(slab_x[side])
            def _():
                for c in xs:
                    c.start()

            @pl.when(slab_y[side])
            def _():
                for c in ys:
                    c.start()

        for ref in (r_ex, r_ey, r_ax, r_ay, r_c0, r_c1):
            ref[...] = jnp.zeros(ref.shape, jnp.float32)

        barrier = pltpu.get_barrier_semaphore()
        for present, target in links:

            @pl.when(present)
            def _():
                pl.semaphore_signal(barrier, inc=1, device_id=target, device_id_type=MESH)

        zero = jnp.zeros((SUB, depth_z), jnp.float32)
        for side in (0, 1):

            @pl.when(jnp.logical_not(slab_x[side]))
            def _():
                @pl.loop(side * PML, side * PML + PML)
                def _(i):
                    for s in (3, 4, 9, 10):
                        S[s, i] = jnp.zeros((rows_y, depth_z), jnp.float32)

            @pl.when(jnp.logical_not(slab_y[side]))
            def _():
                @pl.loop(0, rows_x)
                def _(i):
                    for s in (0, 5, 6, 11):
                        S[s, i, pl.ds(side * PML, PML), :] = jnp.zeros(
                            (PML, depth_z), jnp.float32
                        )

        for c in range(3):
            for t in range(tiles):
                E[c, rows_x, pl.ds(t * SUB, SUB), :] = zero
                H[c, 0, pl.ds(SUB + t * SUB, SUB), :] = zero

        @pl.loop(0, rows_x)
        def _(i):
            for c in range(3):
                E[c, i, pl.ds(rows_y, SUB), :] = zero
                H[c, i + 1, pl.ds(0, SUB), :] = zero

        lane = lax.broadcasted_iota(jnp.int32, (SUB, depth_z), 1)
        row = lax.broadcasted_iota(jnp.int32, (rows_y, depth_z), 0)
        plane = lax.broadcasted_iota(jnp.int32, (rows_x, SUB, depth_z), 0)
        zc = []
        for k, shift in enumerate((0.5, 0.0)):
            zc.append(profile(lane, depth_z, shift))
            for n, v in enumerate(profile(row + gy * rows_y, size_y * rows_y, shift)):
                cy[k, n] = v
            for n, v in enumerate(profile(plane + gx * rows_x, size_x * rows_x, shift)):
                cx[k, n] = v
        not_last = lane < depth_z - 1
        not_first = lane > 0

        keep_vals, drive_vals = [], []
        for m in range(NMAT):
            eps = jnp.full((SUB, depth_z), eps_ref[m], jnp.float32)
            sig = jnp.full((SUB, depth_z), sig_ref[m], jnp.float32)
            loss = sig * time_step / (2.0 * eps)
            keep_vals.append((1.0 - loss) / (1.0 + loss))
            drive_vals.append((time_step / eps) / (1.0 + loss))
        copies[2].wait()

        @pl.loop(0, rows_x)
        def _(i):
            for t in range(tiles):
                rows = pl.ds(t * SUB, SUB)
                number = mat[i, rows, :]
                kv, dv = keep_vals[0], drive_vals[0]
                for m in range(1, NMAT):
                    chosen = number == m
                    kv = jnp.where(chosen, keep_vals[m], kv)
                    dv = jnp.where(chosen, drive_vals[m], dv)
                keep[i, rows, :] = kv
                drive[i, rows, :] = dv

        for n in (0, 1, 3, 4):
            copies[n].wait()
        for side in (0, 1):
            xs, ys = slab_copies(side)

            @pl.when(slab_x[side])
            def _():
                for c in xs:
                    c.wait()

            @pl.when(slab_y[side])
            def _():
                for c in ys:
                    c.wait()

        pl.semaphore_wait(barrier, sum(jnp.where(present, 1, 0) for present, _t in links))

        def term(old, d, coef):
            b, a, q = coef
            renewed = b * old + a * d
            return q * d + renewed, renewed

        def loads(k, i, y, in_x, in_y):
            rows, at = pl.ds(y, SUB), pl.ds(y + SUB, SUB)
            first = 6 * k
            if k == 0:
                src, j, now, step, line = E, i, rows, 1, pl.ds(y + 1, SUB)
                old = [H[c, i + 1, at, :] for c in range(3)]
                mats = ()
            else:
                src, j, now, step, line = H, i + 1, at, -1, pl.ds(y + SUB - 1, SUB)
                old = [E[c, i, rows, :] for c in range(3)]
                mats = (keep[i, rows, :], drive[i, rows, :])
            own = [src[c, j, now, :] for c in range(3)]
            side_x = [src[c, j + step, now, :] for c in (1, 2)]
            side_y = [src[c, j, line, :] for c in (0, 2)]
            slots = [1, 2] + ([3, 4] if in_x else []) + ([0, 5] if in_y else [])
            aux = {n: S[first + n, i, rows, :] for n in slots}
            coef_x = [cx[k, n, i] for n in range(3)] if in_x else None
            return own, side_x, side_y, old, mats, aux, coef_x

        def compute(k, values, coef_y):
            own, (x1, x2), (y0, y2), old, mats, aux, coef_x = values
            f0, f1, f2 = own
            if k == 0:
                dx1, dx2, dy0, dy2 = x1 - f1, x2 - f2, y0 - f0, y2 - f2
                dz0 = jnp.where(not_last, pltpu.roll(f0, depth_z - 1, 1), 0.0) - f0
                dz1 = jnp.where(not_last, pltpu.roll(f1, depth_z - 1, 1), 0.0) - f1
            else:
                dx1, dx2, dy0, dy2 = f1 - x1, f2 - x2, f0 - y0, f2 - y2
                dz0 = f0 - jnp.where(not_first, pltpu.roll(f0, 1, 1), 0.0)
                dz1 = f1 - jnp.where(not_first, pltpu.roll(f1, 1, 1), 0.0)
            fresh = {}
            dz1, fresh[1] = term(aux[1], dz1, zc[k])
            dz0, fresh[2] = term(aux[2], dz0, zc[k])
            if coef_x is not None:
                dx2, fresh[3] = term(aux[3], dx2, coef_x)
                dx1, fresh[4] = term(aux[4], dx1, coef_x)
            if coef_y is not None:
                dy2, fresh[0] = term(aux[0], dy2, coef_y)
                dy0, fresh[5] = term(aux[5], dy0, coef_y)
            curls = (dy2 - dz1, dz0 - dx2, dx1 - dy0)
            if k == 0:
                return [o - time_step * c for o, c in zip(old, curls)], fresh
            return [mats[0] * o + mats[1] * c for o, c in zip(old, curls)], fresh

        def stores(k, i, y, result):
            fields, fresh = result
            for c in range(3):
                if k == 0:
                    H[c, i + 1, pl.ds(y + SUB, SUB), :] = fields[c]
                else:
                    E[c, i, pl.ds(y, SUB), :] = fields[c]
            for n, v in fresh.items():
                S[6 * k + n, i, pl.ds(y, SUB), :] = v

        def run(k, i0, y, in_x, in_y):
            coef_y = [cy[k, n, pl.ds(y, SUB), :] for n in range(3)] if in_y else None
            ready = [loads(k, i0 + u, y, in_x, in_y) for u in range(AHEAD)]
            for u in range(GROUP):
                if u + AHEAD < GROUP:
                    ready.append(loads(k, i0 + u + AHEAD, y, in_x, in_y))
                stores(k, i0 + u, y, compute(k, ready[u], coef_y))

        def unit(k, g, t):
            low_x, low_y = g * GROUP < PML, t * SUB < PML
            px = jnp.where(low_x, slab_x[0], slab_x[1])
            py = jnp.where(low_y, slab_y[0], slab_y[1])
            i0, y = g * GROUP, pl.multiple_of(t * SUB, SUB)

            def split_y(in_x):
                lax.cond(
                    py,
                    lambda: run(k, i0, y, in_x, True),
                    lambda: run(k, i0, y, in_x, False),
                )

            lax.cond(px, lambda: split_y(True), lambda: split_y(False))

        def exchange(s):
            moves = (
                (has_lx, (lx, gy), has_hx, t_ex, r_ex),
                (has_ly, (gx, ly), has_hy, t_ey, r_ey),
                (both(has_hx, has_ly), (hx, ly), both(has_lx, has_hy), t_c0, r_c0),
                (both(has_lx, has_hy), (lx, hy), both(has_hx, has_ly), t_c1, r_c1),
                (has_hx, (hx, gy), has_lx, t_ax, r_ax),
                (has_hy, (gx, hy), has_ly, t_ay, r_ay),
            )
            return [
                (
                    sends,
                    gets,
                    pltpu.make_async_remote_copy(
                        src_ref=src,
                        dst_ref=dst.at[s],
                        send_sem=send_sem.at[n],
                        recv_sem=recv_sem.at[n, s],
                        device_id=target,
                        device_id_type=MESH,
                    ),
                )
                for n, (sends, target, gets, src, dst) in enumerate(moves)
            ]

        own = pl.ds(0, rows_y)
        inner = pl.ds(SUB, rows_y)

        def advance(step, carry):
            s = lax.rem(step, 2)
            moves = exchange(s)
            t_ex[0] = E[1, 0, own, :]
            t_ex[1] = E[2, 0, own, :]
            t_c0[...] = E[0, top, pl.ds(0, SUB), :]
            t_c1[...] = E[1, 0, pl.ds(rows_y - SUB, SUB), :]
            for i in range(rows_x):
                t_ey[0, pl.ds(i, 1), :] = E[0, i, pl.ds(0, 1), :]
                t_ey[1, pl.ds(i, 1), :] = E[2, i, pl.ds(0, 1), :]
            for sends, _g, copy in moves[:4]:

                @pl.when(sends)
                def _():
                    copy.start()

            @pl.loop(0, tiles + groups - 1)
            def _(k):
                face = k < tiles
                unit(
                    0, jnp.where(face, groups - 1, k - tiles), jnp.where(face, k, tiles - 1)
                )

            t_ax[0] = H[1, rows_x, inner, :]
            t_ax[1] = H[2, rows_x, inner, :]
            for i in range(rows_x):
                t_ay[0, pl.ds(i, 1), :] = H[0, i + 1, pl.ds(SUB + right, 1), :]
                t_ay[1, pl.ds(i, 1), :] = H[2, i + 1, pl.ds(SUB + right, 1), :]
            for sends, _g, copy in moves[4:]:

                @pl.when(sends)
                def _():
                    copy.start()

            @pl.loop(0, (groups - 1) * (tiles - 1))
            def _(k):
                unit(0, lax.div(k, tiles - 1), lax.rem(k, tiles - 1))

            @pl.loop(0, (groups - 2) * (tiles - 2))
            def _(k):
                unit(1, 1 + lax.div(k, tiles - 2), 1 + lax.rem(k, tiles - 2))

            for _s, gets, copy in moves:

                @pl.when(gets)
                def _():
                    copy.wait_recv()

            half = time_step

            @pl.when(has_hx)
            def _():
                H[1, rows_x, inner, :] = H[1, rows_x, inner, :] + half * r_ex[s, 1]
                H[2, rows_x, inner, :] = H[2, rows_x, inner, :] - half * r_ex[s, 0]

            @pl.when(has_hy)
            def _():
                edge = pl.ds(SUB + right, 1)
                for i in range(rows_x):
                    H[0, i + 1, edge, :] = (
                        H[0, i + 1, edge, :] - half * r_ey[s, 1, pl.ds(i, 1), :]
                    )
                    H[2, i + 1, edge, :] = (
                        H[2, i + 1, edge, :] + half * r_ey[s, 0, pl.ds(i, 1), :]
                    )

            @pl.when(has_lx)
            def _():
                H[1, 0, inner, :] = r_ax[s, 0] + half * E[2, 0, own, :]
                H[2, 0, inner, :] = r_ax[s, 1] - half * E[1, 0, own, :]
                edge = pl.ds(SUB + right, 1)
                H[2, 0, edge, :] = H[2, 0, edge, :] + half * r_c0[s, pl.ds(0, 1), :]

            @pl.when(has_ly)
            def _():
                edge = pl.ds(SUB - 1, 1)
                first = pl.ds(0, 1)
                for i in range(rows_x):
                    line = pl.ds(i, 1)
                    H[0, i + 1, edge, :] = r_ay[s, 0, line, :] - half * E[2, i, first, :]
                    H[2, i + 1, edge, :] = r_ay[s, 1, line, :] + half * E[0, i, first, :]
                H[2, rows_x, edge, :] = (
                    H[2, rows_x, edge, :] - half * r_c1[s, pl.ds(SUB - 1, 1), :]
                )

            @pl.loop(0, 2 * groups + 2 * (tiles - 2))
            def _(k):
                side = k < 2 * groups
                j = k - 2 * groups
                g = jnp.where(side, lax.rem(k, groups), (groups - 1) * lax.rem(j, 2))
                t = jnp.where(side, (tiles - 1) * lax.div(k, groups), 1 + lax.div(j, 2))
                unit(1, g, t)

            for sends, _g, copy in moves:

                @pl.when(sends)
                def _():
                    copy.wait_send()

            return carry

        lax.fori_loop(0, STEPS, advance, 0)

    return kernel


def make_writer(rows_x, rows_y):
    def writer(E, H, S, e_out, h_out, p_out, out_sem):
        outs = [
            pltpu.make_async_copy(
                E.at[:, pl.ds(0, rows_x), pl.ds(0, rows_y), :], e_out, out_sem.at[0]
            ),
            pltpu.make_async_copy(
                H.at[:, pl.ds(1, rows_x), pl.ds(SUB, rows_y), :], h_out, out_sem.at[1]
            ),
            pltpu.make_async_copy(S, p_out, out_sem.at[2]),
        ]
        for c in outs:
            c.start()
        for c in outs:
            c.wait()

    return writer


def solution(mesh):
    size_x, size_y = mesh.shape["gx"], mesh.shape["gy"]

    def shards(e_field, h_field, psi, material, eps_table, sigma_table):
        _, rows_x, rows_y, depth_z = e_field.shape
        assert rows_x == 2 * PML and rows_y == 2 * PML and size_x > 1 and size_y > 1
        f32 = jnp.float32
        any_space = pl.BlockSpec(memory_space=pltpu.HBM)
        smem = pl.BlockSpec(memory_space=pltpu.SMEM)
        face_x = (2, rows_y, depth_z)
        face_y = (2, rows_x, depth_z)
        corner = (SUB, depth_z)
        faces = (face_x, face_y, face_x, face_y, corner, corner)
        padded = (3, rows_x + 1, rows_y + SUB, depth_z)
        cell = (rows_x, rows_y, depth_z)
        vmem = pl.BlockSpec(memory_space=pltpu.VMEM)
        state = pl.pallas_call(
            make_kernel(size_x, size_y, rows_x, rows_y, depth_z),
            out_shape=[pltpu.VMEM(padded, f32), pltpu.VMEM(padded, f32), pltpu.VMEM(psi.shape, f32)],
            in_specs=[any_space] * 4 + [smem] * 2,
            out_specs=[vmem] * 3,
            scratch_shapes=[
                pltpu.VMEM(cell, f32),
                pltpu.VMEM(cell, f32),
                pltpu.VMEM(cell, jnp.int32),
                pltpu.VMEM((2, 3, rows_x, SUB, depth_z), f32),
                pltpu.VMEM((2, 3, rows_y, depth_z), f32),
            ]
            + [pltpu.VMEM(f, f32) for f in faces]
            + [pltpu.VMEM((2,) + f, f32) for f in faces]
            + [
                pltpu.SemaphoreType.DMA((11,)),
                pltpu.SemaphoreType.DMA((6,)),
                pltpu.SemaphoreType.DMA((6, 2)),
            ],
            compiler_params=pltpu.CompilerParams(
                collective_id=0, has_side_effects=True, vmem_limit_bytes=53 << 20
            ),
        )(e_field, h_field, psi, material, eps_table, sigma_table)
        return pl.pallas_call(
            make_writer(rows_x, rows_y),
            out_shape=[jax.ShapeDtypeStruct(a.shape, f32) for a in (e_field, h_field, psi)],
            in_specs=[vmem] * 3,
            out_specs=[any_space] * 3,
            scratch_shapes=[pltpu.SemaphoreType.DMA((3,))],
            compiler_params=pltpu.CompilerParams(vmem_limit_bytes=24 << 20),
        )(*state)

    split = P(None, "gx", "gy", None)
    return jax.shard_map(
        shards,
        mesh=mesh,
        in_specs=(split, split, split, P("gx", "gy", None), P(), P()),
        out_specs=(split, split, split),
        check_vma=False,
    )
```

profile of v0, /device:TPU:0, one launch (start us, length us, event | category | flops | bytes accessed | tf_op | source)
XLA Modules:
  0.0 92.1 jit_solution(15863414629102009045)
XLA Ops:
  0.6 87.7 %shard_map.85 = (f32[3,33,40,128]{3,2,1,0:T(8,128)S(1)}, f32[3,33,40,128]{3,2,1,0:T(8,128)S(1)}, f32[12,32,32,128]{3,2,1,0:T(8,128)S(1)}) custom-call(f32[3,32,32,128]{3,2,1,0:T(8,128)} %e_in.1, f32[3,32,32,128]{3,2,1,0:T(8,128)} %h_in.1, f32[12,32,32,128]{3,2,1,0:T(8,128)} %p_in.1, s32[32,32,128]{2,1,0:T(8,128)} %m_in.1, f32[8]{0:T(128)} %eps_ref.1, f32[8]{0:T(128)} %sig_ref.1), custom_call_target="tpu_custom_call" | custom-call | tf_op jit(solution)/shard_map/pallas_call | solution.py:458
  88.3 3.8 %shard_map.86 = (f32[3,32,32,128]{3,2,1,0:T(8,128)}, f32[3,32,32,128]{3,2,1,0:T(8,128)}, f32[12,32,32,128]{3,2,1,0:T(8,128)}) custom-call(f32[3,33,40,128]{3,2,1,0:T(8,128)S(1)} %get-tuple-element.6.E, f32[3,33,40,128]{3,2,1,0:T(8,128)S(1)} %get-tuple-element.7.H, f32[12,32,32,128]{3,2,1,0:T(8,128)S(1)} %get-tuple-element.8.S), custom_call_target="tpu_custom_call" | custom-call | tf_op jit(solution)/shard_map/pallas_call | solution.py:481
where the time goes:
time: 92.3 us; the launch traced here: 92.1 us
  Pallas kernels  91.5 us (99%)
    pallas_call x1, Pallas kernels, shards(): pl.pallas_call(make_kernel(size_x, size_y, rows_x, rows_y, depth_z), out_...  87.7 us
    pallas_call x1, Pallas kernels, shards(): pl.pallas_call(make_writer(rows_x, rows_y), out_shape=[jax.ShapeDtypeStru...  3.77 us

commit v1 on v0

--- a/solution.py
+++ b/solution.py
@@ -51,7 +51,7 @@
 
     def kernel(
         e_in, h_in, p_in, m_in, eps_ref, sig_ref, E, H, S,
-        keep, drive, mat, cx, cy,
+        keep, drive, mat, cx, cy, cp, edge_x, edge_y,
         t_ex, t_ey, t_ax, t_ay, t_c0, t_c1,
         r_ex, r_ey, r_ax, r_ay, r_c0, r_c1,
         in_sem, send_sem, recv_sem,
@@ -154,6 +154,7 @@
 
         lane = lax.broadcasted_iota(jnp.int32, (SUB, depth_z), 1)
         row = lax.broadcasted_iota(jnp.int32, (rows_y, depth_z), 0)
+        column = lax.broadcasted_iota(jnp.int32, (rows_x, depth_z), 0)
         plane = lax.broadcasted_iota(jnp.int32, (rows_x, SUB, depth_z), 0)
         zc = []
         for k, shift in enumerate((0.5, 0.0)):
@@ -162,6 +163,8 @@
                 cy[k, n] = v
             for n, v in enumerate(profile(plane + gx * rows_x, size_x * rows_x, shift)):
                 cx[k, n] = v
+            for n, v in enumerate(profile(column + gx * rows_x, size_x * rows_x, shift)):
+                cp[k, n] = v
         not_last = lane < depth_z - 1
         not_first = lane > 0
 
@@ -289,13 +292,13 @@
         def exchange(s):
             moves = (
                 (has_lx, (lx, gy), has_hx, t_ex, r_ex),
-                (has_ly, (gx, ly), has_hy, t_ey, r_ey),
+                (has_hx, (hx, gy), has_lx, t_ax, r_ax),
                 (both(has_hx, has_ly), (hx, ly), both(has_lx, has_hy), t_c0, r_c0),
                 (both(has_lx, has_hy), (lx, hy), both(has_hx, has_ly), t_c1, r_c1),
-                (has_hx, (hx, gy), has_lx, t_ax, r_ax),
+                (has_ly, (gx, ly), has_hy, t_ey, r_ey),
                 (has_hy, (gx, hy), has_ly, t_ay, r_ay),
             )
-            return [
+            made = [
                 (
                     sends,
                     gets,
@@ -310,75 +313,140 @@
                 )
                 for n, (sends, target, gets, src, dst) in enumerate(moves)
             ]
+            return made[:4], made[4:]
 
         own = pl.ds(0, rows_y)
         inner = pl.ds(SUB, rows_y)
-
-        def advance(step, carry):
-            s = lax.rem(step, 2)
-            moves = exchange(s)
-            t_ex[0] = E[1, 0, own, :]
-            t_ex[1] = E[2, 0, own, :]
-            t_c0[...] = E[0, top, pl.ds(0, SUB), :]
-            t_c1[...] = E[1, 0, pl.ds(rows_y - SUB, SUB), :]
-            for i in range(rows_x):
-                t_ey[0, pl.ds(i, 1), :] = E[0, i, pl.ds(0, 1), :]
-                t_ey[1, pl.ds(i, 1), :] = E[2, i, pl.ds(0, 1), :]
-            for sends, _g, copy in moves[:4]:
+        half = time_step
+        wide = rows_y + SUB
+        flat_e = E.reshape(3 * (rows_x + 1) * wide, depth_z)
+        flat_h = H.reshape(3 * (rows_x + 1) * wide, depth_z)
+        flat_s = S.reshape(12 * rows_x * rows_y, depth_z)
+        flat_keep = keep.reshape(rows_x * rows_y, depth_z)
+        flat_drive = drive.reshape(rows_x * rows_y, depth_z)
+        packs = rows_x // SUB
+
+        def across(c, i, y):
+            return pl.ds((c * (rows_x + 1) + i) * wide + y, SUB, stride=wide)
+
+        def within(c, i, y):
+            return pl.ds((c * rows_x + i) * rows_y + y, SUB, stride=rows_y)
+
+        def start(moves):
+            for sends, _g, copy in moves:
 
                 @pl.when(sends)
                 def _():
                     copy.start()
 
-            @pl.loop(0, tiles + groups - 1)
-            def _(k):
-                face = k < tiles
-                unit(
-                    0, jnp.where(face, groups - 1, k - tiles), jnp.where(face, k, tiles - 1)
-                )
-
-            t_ax[0] = H[1, rows_x, inner, :]
-            t_ax[1] = H[2, rows_x, inner, :]
-            for i in range(rows_x):
-                t_ay[0, pl.ds(i, 1), :] = H[0, i + 1, pl.ds(SUB + right, 1), :]
-                t_ay[1, pl.ds(i, 1), :] = H[2, i + 1, pl.ds(SUB + right, 1), :]
-            for sends, _g, copy in moves[4:]:
-
-                @pl.when(sends)
-                def _():
-                    copy.start()
-
-            @pl.loop(0, (groups - 1) * (tiles - 1))
-            def _(k):
-                unit(0, lax.div(k, tiles - 1), lax.rem(k, tiles - 1))
-
-            @pl.loop(0, (groups - 2) * (tiles - 2))
-            def _(k):
-                unit(1, 1 + lax.div(k, tiles - 2), 1 + lax.rem(k, tiles - 2))
-
-            for _s, gets, copy in moves:
+        def finish(moves):
+            for sends, gets, copy in moves:
 
                 @pl.when(gets)
                 def _():
                     copy.wait_recv()
 
-            half = time_step
+                @pl.when(sends)
+                def _():
+                    copy.wait_send()
+
+        def coefs_y(k, y):
+            return [cy[k, n, pl.ds(y, SUB), :] for n in range(3)]
+
+        def faces_x():
+            late = []
+            for t in range(tiles):
+                y = t * SUB
+                fields, _f = compute(1, loads(1, 0, y, False, True), coefs_y(1, y))
+                t_ex[0, pl.ds(y, SUB), :] = fields[1]
+                t_ex[1, pl.ds(y, SUB), :] = fields[2]
+                if t == tiles - 1:
+                    t_c1[...] = fields[1]
+                fields, _f = compute(1, loads(1, top, y, False, True), coefs_y(1, y))
+                edge_x[pl.ds(y, SUB), :] = fields[0]
+                if t == 0:
+                    t_c0[...] = fields[0]
+                late.append(fields)
+            for t in range(tiles):
+                y = t * SUB
+                rows, at = pl.ds(y, SUB), pl.ds(y + SUB, SUB)
+                old = [H[c, rows_x, at, :] for c in range(3)]
+                aux = {n: S[n, top, rows, :] for n in (1, 2, 0, 5)}
+                side_y = (edge_x[pl.ds(y + 1, SUB), :], zero)
+                values = (late[t], (zero, zero), side_y, old, (), aux, None)
+                fields, _f = compute(0, values, coefs_y(0, y))
+                t_ax[0, rows, :] = fields[1]
+                t_ax[1, rows, :] = fields[2]
+
+        def packed_e(r, u):
+            i = u * SUB
+            own_h = [flat_h[across(c, i + 1, SUB + r), :] for c in range(3)]
+            side_x = [flat_h[across(c, i, SUB + r), :] for c in (1, 2)]
+            side_y = [flat_h[across(c, i + 1, SUB + r - 1), :] for c in (0, 2)]
+            old = [flat_e[across(c, i, r), :] for c in range(3)]
+            mats = (flat_keep[within(0, i, r), :], flat_drive[within(0, i, r), :])
+            aux = {n: flat_s[within(6 + n, i, r), :] for n in (1, 2, 3, 4)}
+            coef_x = [cp[1, n, pl.ds(i, SUB), :] for n in range(3)]
+            return compute(1, (own_h, side_x, side_y, old, mats, aux, coef_x), None)[0]
+
+        def faces_y():
+            late = []
+            for u in range(packs):
+                rows = pl.ds(u * SUB, SUB)
+                fields = packed_e(0, u)
+                t_ey[0, rows, :] = fields[0]
+                t_ey[1, rows, :] = fields[2]
+                fields = packed_e(right, u)
+                edge_y[rows, :] = fields[1]
+                late.append(fields)
+            for u in range(packs):
+                i = u * SUB
+                rows = pl.ds(i, SUB)
+                old = [flat_h[across(c, i + 1, SUB + right), :] for c in range(3)]
+                aux = {n: flat_s[within(n, i, right), :] for n in (1, 2, 3, 4)}
+                coef_x = [cp[0, n, rows, :] for n in range(3)]
+                side_x = (edge_y[pl.ds(i + 1, SUB), :], zero)
+                values = (late[u], side_x, (zero, zero), old, (), aux, coef_x)
+                fields, _f = compute(0, values, None)
+                t_ay[0, rows, :] = fields[0]
+                t_ay[1, rows, :] = fields[2]
+
+        def sweep(k, count):
+            @pl.loop(0, count)
+            def _(n):
+                unit(k, lax.div(n, tiles), lax.rem(n, tiles))
+
+        def fix_y(s):
+            @pl.when(has_hy)
+            def _():
+                for u in range(packs):
+                    i = u * SUB
+                    rows = pl.ds(i, SUB)
+                    a0, a2 = across(0, i + 1, SUB + right), across(2, i + 1, SUB + right)
+                    flat_h[a0, :] = flat_h[a0, :] - half * r_ey[s, 1, rows, :]
+                    flat_h[a2, :] = flat_h[a2, :] + half * r_ey[s, 0, rows, :]
+
+            @pl.when(has_ly)
+            def _():
+                for u in range(packs):
+                    i = u * SUB
+                    rows = pl.ds(i, SUB)
+                    e0, e2 = flat_e[across(0, i, 0), :], flat_e[across(2, i, 0), :]
+                    flat_h[across(0, i + 1, SUB - 1), :] = r_ay[s, 0, rows, :] - half * e2
+                    flat_h[across(2, i + 1, SUB - 1), :] = r_ay[s, 1, rows, :] + half * e0
+
+        def fix_x(s):
+            @pl.when(has_ly)
+            def _():
+                edge = pl.ds(SUB - 1, 1)
+                H[2, rows_x, edge, :] = (
+                    H[2, rows_x, edge, :] - half * r_c1[s, pl.ds(SUB - 1, 1), :]
+                )
 
             @pl.when(has_hx)
             def _():
                 H[1, rows_x, inner, :] = H[1, rows_x, inner, :] + half * r_ex[s, 1]
                 H[2, rows_x, inner, :] = H[2, rows_x, inner, :] - half * r_ex[s, 0]
-
-            @pl.when(has_hy)
-            def _():
-                edge = pl.ds(SUB + right, 1)
-                for i in range(rows_x):
-                    H[0, i + 1, edge, :] = (
-                        H[0, i + 1, edge, :] - half * r_ey[s, 1, pl.ds(i, 1), :]
-                    )
-                    H[2, i + 1, edge, :] = (
-                        H[2, i + 1, edge, :] + half * r_ey[s, 0, pl.ds(i, 1), :]
-                    )
 
             @pl.when(has_lx)
             def _():
@@ -387,32 +455,46 @@
                 edge = pl.ds(SUB + right, 1)
                 H[2, 0, edge, :] = H[2, 0, edge, :] + half * r_c0[s, pl.ds(0, 1), :]
 
-            @pl.when(has_ly)
-            def _():
-                edge = pl.ds(SUB - 1, 1)
-                first = pl.ds(0, 1)
-                for i in range(rows_x):
-                    line = pl.ds(i, 1)
-                    H[0, i + 1, edge, :] = r_ay[s, 0, line, :] - half * E[2, i, first, :]
-                    H[2, i + 1, edge, :] = r_ay[s, 1, line, :] + half * E[0, i, first, :]
-                H[2, rows_x, edge, :] = (
-                    H[2, rows_x, edge, :] - half * r_c1[s, pl.ds(SUB - 1, 1), :]
-                )
-
-            @pl.loop(0, 2 * groups + 2 * (tiles - 2))
-            def _(k):
-                side = k < 2 * groups
-                j = k - 2 * groups
-                g = jnp.where(side, lax.rem(k, groups), (groups - 1) * lax.rem(j, 2))
-                t = jnp.where(side, (tiles - 1) * lax.div(k, groups), 1 + lax.div(j, 2))
-                unit(1, g, t)
-
-            for sends, _g, copy in moves:
-
-                @pl.when(sends)
-                def _():
-                    copy.wait_send()
-
+        edge_x[pl.ds(rows_y, SUB), :] = zero
+        edge_y[pl.ds(rows_x, SUB), :] = zero
+        count = groups * tiles
+        sweep(0, count)
+        t_ex[0] = E[1, 0, own, :]
+        t_ex[1] = E[2, 0, own, :]
+        t_ax[0] = H[1, rows_x, inner, :]
+        t_ax[1] = H[2, rows_x, inner, :]
+        t_c0[...] = E[0, top, pl.ds(0, SUB), :]
+        t_c1[...] = E[1, 0, pl.ds(rows_y - SUB, SUB), :]
+        for u in range(packs):
+            i = u * SUB
+            rows = pl.ds(i, SUB)
+            t_ey[0, rows, :] = flat_e[across(0, i, 0), :]
+            t_ey[1, rows, :] = flat_e[across(2, i, 0), :]
+            t_ay[0, rows, :] = flat_h[across(0, i + 1, SUB + right), :]
+            t_ay[1, rows, :] = flat_h[across(2, i + 1, SUB + right), :]
+        first_x, first_y = exchange(0)
+        start(first_x)
+        start(first_y)
+
+        def advance(step, carry):
+            s = lax.rem(step, 2)
+            old_x, old_y = exchange(s)
+            new_x, new_y = exchange(1 - s)
+            more = step < STEPS - 1
+            finish(old_y)
+            fix_y(s)
+            finish(old_x)
+            fix_x(s)
+
+            @pl.when(more)
+            def _():
+                faces_x()
+                start(new_x)
+                faces_y()
+                start(new_y)
+
+            sweep(1, count)
+            sweep(0, jnp.where(more, count, 0))
             return carry
 
         lax.fori_loop(0, STEPS, advance, 0)
@@ -466,6 +548,9 @@
                 pltpu.VMEM(cell, jnp.int32),
                 pltpu.VMEM((2, 3, rows_x, SUB, depth_z), f32),
                 pltpu.VMEM((2, 3, rows_y, depth_z), f32),
+                pltpu.VMEM((2, 3, rows_x, depth_z), f32),
+                pltpu.VMEM((rows_y + SUB, depth_z), f32),
+                pltpu.VMEM((rows_x + SUB, depth_z), f32),
             ]
             + [pltpu.VMEM(f, f32) for f in faces]
             + [pltpu.VMEM((2,) + f, f32) for f in faces]

time: 92.3 us -> 74.7 us (0.81)
  Pallas kernels: 91.5 us -> 73.9 us
    pallas_call x1, Pallas kernels: 87.7 us -> 70.2 us  [shards(): pl.pallas_call(make_kernel(size_x, size_y, rows_x, rows_y, depth_z), out_...]
where the time goes in v1:
time: 74.7 us; the launch traced here: 74.6 us
  Pallas kernels  73.9 us (99%)
    pallas_call x1, Pallas kernels, shards(): pl.pallas_call(make_kernel(size_x, size_y, rows_x, rows_y, depth_z), out_...  70.2 us
    pallas_call x1, Pallas kernels, shards(): pl.pallas_call(make_writer(rows_x, rows_y), out_shape=[jax.ShapeDtypeStru...  3.77 us

profile of v1, /device:TPU:0, one launch (start us, length us, event | category | flops | bytes accessed | tf_op | source)
XLA Modules:
  0.0 74.6 jit_solution(4405803215097033758)
XLA Ops:
  0.6 70.2 %shard_map.85 = (f32[3,33,40,128]{3,2,1,0:T(8,128)S(1)}, f32[3,33,40,128]{3,2,1,0:T(8,128)S(1)}, f32[12,32,32,128]{3,2,1,0:T(8,128)S(1)}) custom-call(f32[3,32,32,128]{3,2,1,0:T(8,128)} %e_in.1, f32[3,32,32,128]{3,2,1,0:T(8,128)} %h_in.1, f32[12,32,32,128]{3,2,1,0:T(8,128)} %p_in.1, s32[32,32,128]{2,1,0:T(8,128)} %m_in.1, f32[8]{0:T(128)} %eps_ref.1, f32[8]{0:T(128)} %sig_ref.1), custom_call_target="tpu_custom_call" | custom-call | tf_op jit(solution)/shard_map/pallas_call | solution.py:540
  70.8 3.8 %shard_map.86 = (f32[3,32,32,128]{3,2,1,0:T(8,128)}, f32[3,32,32,128]{3,2,1,0:T(8,128)}, f32[12,32,32,128]{3,2,1,0:T(8,128)}) custom-call(f32[3,33,40,128]{3,2,1,0:T(8,128)S(1)} %get-tuple-element.6.E, f32[3,33,40,128]{3,2,1,0:T(8,128)S(1)} %get-tuple-element.7.H, f32[12,32,32,128]{3,2,1,0:T(8,128)S(1)} %get-tuple-element.8.S), custom_call_target="tpu_custom_call" | custom-call | tf_op jit(solution)/shard_map/pallas_call | solution.py:566

commit v2 on v1

--- a/solution.py
+++ b/solution.py
@@ -72,48 +72,66 @@
             (both(has_lx, has_hy), (lx, hy)),
         )
 
-        plain = [
-            (e_in, E.at[:, pl.ds(0, rows_x), pl.ds(0, rows_y), :]),
-            (h_in, H.at[:, pl.ds(1, rows_x), pl.ds(SUB, rows_y), :]),
-            (m_in, mat),
-            (p_in.at[pl.ds(1, 2)], S.at[pl.ds(1, 2)]),
-            (p_in.at[pl.ds(7, 2)], S.at[pl.ds(7, 2)]),
-        ]
-        copies = [pltpu.make_async_copy(a, b, in_sem.at[n]) for n, (a, b) in enumerate(plain)]
-        for c in copies:
-            c.start()
-
-        def slab_copies(side):
-            half_x = pl.ds(side * PML, PML)
-            xs = [
-                pltpu.make_async_copy(
-                    p_in.at[pl.ds(s, 2), half_x], S.at[pl.ds(s, 2), half_x], in_sem.at[5 + n]
+        def field_copies():
+            pairs = (
+                (e_in, E.at[:, pl.ds(0, rows_x), pl.ds(0, rows_y), :]),
+                (h_in, H.at[:, pl.ds(1, rows_x), pl.ds(SUB, rows_y), :]),
+                (m_in, mat),
+            )
+            return [pltpu.make_async_copy(a, b, in_sem.at[n]) for n, (a, b) in enumerate(pairs)]
+
+        def slot_copies(k):
+            first, base = 6 * k, 3 + 7 * k
+            pair = pl.ds(first + 1, 2)
+            always = pltpu.make_async_copy(p_in.at[pair], S.at[pair], in_sem.at[base])
+            guarded = []
+            for side in (0, 1):
+                half_x, pair = pl.ds(side * PML, PML), pl.ds(first + 3, 2)
+                guarded.append(
+                    (
+                        slab_x[side],
+                        pltpu.make_async_copy(
+                            p_in.at[pair, half_x], S.at[pair, half_x], in_sem.at[base + 1 + side]
+                        ),
+                    )
                 )
-                for n, s in enumerate((3, 9))
-            ]
-            ys = [
-                pltpu.make_async_copy(
-                    p_in.at[s, :, half_x], S.at[s, :, half_x], in_sem.at[7 + n]
-                )
-                for n, s in enumerate((0, 5, 6, 11))
-            ]
-            return xs, ys
-
-        for side in (0, 1):
-            xs, ys = slab_copies(side)
-
-            @pl.when(slab_x[side])
-            def _():
-                for c in xs:
-                    c.start()
-
-            @pl.when(slab_y[side])
-            def _():
-                for c in ys:
-                    c.start()
-
-        for ref in (r_ex, r_ey, r_ax, r_ay, r_c0, r_c1):
-            ref[...] = jnp.zeros(ref.shape, jnp.float32)
+                for n, slot in enumerate((first, first + 5)):
+                    guarded.append(
+                        (
+                            slab_y[side],
+                            pltpu.make_async_copy(
+                                p_in.at[slot, :, half_x],
+                                S.at[slot, :, half_x],
+                                in_sem.at[base + 3 + 2 * side + n],
+                            ),
+                        )
+                    )
+            return always, guarded
+
+        def start_slots(k):
+            always, guarded = slot_copies(k)
+            always.start()
+            for present, copy in guarded:
+
+                @pl.when(present)
+                def _():
+                    copy.start()
+
+        def wait_slots(k):
+            always, guarded = slot_copies(k)
+            always.wait()
+            for present, copy in guarded:
+
+                @pl.when(present)
+                def _():
+                    copy.wait()
+
+        fields_in = field_copies()
+        fields_in[0].start()
+        fields_in[1].start()
+        start_slots(0)
+        fields_in[2].start()
+        start_slots(1)
 
         barrier = pltpu.get_barrier_semaphore()
         for present, target in links:
@@ -168,44 +186,27 @@
         not_last = lane < depth_z - 1
         not_first = lane > 0
 
-        keep_vals, drive_vals = [], []
-        for m in range(NMAT):
-            eps = jnp.full((SUB, depth_z), eps_ref[m], jnp.float32)
-            sig = jnp.full((SUB, depth_z), sig_ref[m], jnp.float32)
-            loss = sig * time_step / (2.0 * eps)
-            keep_vals.append((1.0 - loss) / (1.0 + loss))
-            drive_vals.append((time_step / eps) / (1.0 + loss))
-        copies[2].wait()
-
-        @pl.loop(0, rows_x)
-        def _(i):
-            for t in range(tiles):
-                rows = pl.ds(t * SUB, SUB)
-                number = mat[i, rows, :]
-                kv, dv = keep_vals[0], drive_vals[0]
-                for m in range(1, NMAT):
-                    chosen = number == m
-                    kv = jnp.where(chosen, keep_vals[m], kv)
-                    dv = jnp.where(chosen, drive_vals[m], dv)
-                keep[i, rows, :] = kv
-                drive[i, rows, :] = dv
-
-        for n in (0, 1, 3, 4):
-            copies[n].wait()
-        for side in (0, 1):
-            xs, ys = slab_copies(side)
-
-            @pl.when(slab_x[side])
-            def _():
-                for c in xs:
-                    c.wait()
-
-            @pl.when(slab_y[side])
-            def _():
-                for c in ys:
-                    c.wait()
-
-        pl.semaphore_wait(barrier, sum(jnp.where(present, 1, 0) for present, _t in links))
+        def materials():
+            keep_vals, drive_vals = [], []
+            for m in range(NMAT):
+                eps = jnp.full((SUB, depth_z), eps_ref[m], jnp.float32)
+                sig = jnp.full((SUB, depth_z), sig_ref[m], jnp.float32)
+                loss = sig * time_step / (2.0 * eps)
+                keep_vals.append((1.0 - loss) / (1.0 + loss))
+                drive_vals.append((time_step / eps) / (1.0 + loss))
+
+            @pl.loop(0, rows_x)
+            def _(i):
+                for t in range(tiles):
+                    rows = pl.ds(t * SUB, SUB)
+                    number = mat[i, rows, :]
+                    kv, dv = keep_vals[0], drive_vals[0]
+                    for m in range(1, NMAT):
+                        chosen = number == m
+                        kv = jnp.where(chosen, keep_vals[m], kv)
+                        dv = jnp.where(chosen, drive_vals[m], dv)
+                    keep[i, rows, :] = kv
+                    drive[i, rows, :] = dv
 
         def term(old, d, coef):
             b, a, q = coef
@@ -290,13 +291,15 @@
             lax.cond(px, lambda: split_y(True), lambda: split_y(False))
 
         def exchange(s):
+            one, last = pl.ds(0, 1), pl.ds(SUB - 1, 1)
+            diag_c0, diag_c1 = both(has_hx, has_ly), both(has_lx, has_hy)
             moves = (
-                (has_lx, (lx, gy), has_hx, t_ex, r_ex),
-                (has_hx, (hx, gy), has_lx, t_ax, r_ax),
-                (both(has_hx, has_ly), (hx, ly), both(has_lx, has_hy), t_c0, r_c0),
-                (both(has_lx, has_hy), (lx, hy), both(has_hx, has_ly), t_c1, r_c1),
-                (has_ly, (gx, ly), has_hy, t_ey, r_ey),
-                (has_hy, (gx, hy), has_ly, t_ay, r_ay),
+                (diag_c0, (hx, ly), diag_c1, t_c0.at[one], r_c0.at[s, one]),
+                (has_hx, (hx, gy), has_lx, t_ax, r_ax.at[s]),
+                (diag_c1, (lx, hy), diag_c0, t_c1.at[last], r_c1.at[s, last]),
+                (has_lx, (lx, gy), has_hx, t_ex, r_ex.at[s]),
+                (has_ly, (gx, ly), has_hy, t_ey, r_ey.at[s]),
+                (has_hy, (gx, hy), has_ly, t_ay, r_ay.at[s]),
             )
             made = [
                 (
@@ -304,7 +307,7 @@
                     gets,
                     pltpu.make_async_remote_copy(
                         src_ref=src,
-                        dst_ref=dst.at[s],
+                        dst_ref=dst,
                         send_sem=send_sem.at[n],
                         recv_sem=recv_sem.at[n, s],
                         device_id=target,
@@ -313,7 +316,7 @@
                 )
                 for n, (sends, target, gets, src, dst) in enumerate(moves)
             ]
-            return made[:4], made[4:]
+            return made[:2], made[2:4], made[4:]
 
         own = pl.ds(0, rows_y)
         inner = pl.ds(SUB, rows_y)
@@ -339,13 +342,16 @@
                 def _():
                     copy.start()
 
-        def finish(moves):
-            for sends, gets, copy in moves:
+        def arrived(moves):
+            for _s, gets, copy in moves:
 
                 @pl.when(gets)
                 def _():
                     copy.wait_recv()
 
+        def left(moves):
+            for sends, _g, copy in moves:
+
                 @pl.when(sends)
                 def _():
                     copy.wait_send()
@@ -353,8 +359,7 @@
         def coefs_y(k, y):
             return [cy[k, n, pl.ds(y, SUB), :] for n in range(3)]
 
-        def faces_x():
-            late = []
+        def face_low():
             for t in range(tiles):
                 y = t * SUB
                 fields, _f = compute(1, loads(1, 0, y, False, True), coefs_y(1, y))
@@ -362,18 +367,25 @@
                 t_ex[1, pl.ds(y, SUB), :] = fields[2]
                 if t == tiles - 1:
                     t_c1[...] = fields[1]
-                fields, _f = compute(1, loads(1, top, y, False, True), coefs_y(1, y))
-                edge_x[pl.ds(y, SUB), :] = fields[0]
-                if t == 0:
-                    t_c0[...] = fields[0]
-                late.append(fields)
+
+        def face_high():
+            fields = []
+            for t in range(tiles):
+                y = t * SUB
+                fields.append(compute(1, loads(1, top, y, False, True), coefs_y(1, y))[0])
+            partial_high(fields)
+
+        def partial_high(e_new):
+            t_c0[...] = e_new[0][0]
+            for t in range(tiles):
+                edge_x[pl.ds(t * SUB, SUB), :] = e_new[t][0]
             for t in range(tiles):
                 y = t * SUB
                 rows, at = pl.ds(y, SUB), pl.ds(y + SUB, SUB)
                 old = [H[c, rows_x, at, :] for c in range(3)]
                 aux = {n: S[n, top, rows, :] for n in (1, 2, 0, 5)}
                 side_y = (edge_x[pl.ds(y + 1, SUB), :], zero)
-                values = (late[t], (zero, zero), side_y, old, (), aux, None)
+                values = (e_new[t], (zero, zero), side_y, old, (), aux, None)
                 fields, _f = compute(0, values, coefs_y(0, y))
                 t_ax[0, rows, :] = fields[1]
                 t_ax[1, rows, :] = fields[2]
@@ -396,9 +408,12 @@
                 fields = packed_e(0, u)
                 t_ey[0, rows, :] = fields[0]
                 t_ey[1, rows, :] = fields[2]
-                fields = packed_e(right, u)
-                edge_y[rows, :] = fields[1]
-                late.append(fields)
+                late.append(packed_e(right, u))
+            partial_y(late)
+
+        def partial_y(e_new):
+            for u in range(packs):
+                edge_y[pl.ds(u * SUB, SUB), :] = e_new[u][1]
             for u in range(packs):
                 i = u * SUB
                 rows = pl.ds(i, SUB)
@@ -406,7 +421,7 @@
                 aux = {n: flat_s[within(n, i, right), :] for n in (1, 2, 3, 4)}
                 coef_x = [cp[0, n, rows, :] for n in range(3)]
                 side_x = (edge_y[pl.ds(i + 1, SUB), :], zero)
-                values = (late[u], side_x, (zero, zero), old, (), aux, coef_x)
+                values = (e_new[u], side_x, (zero, zero), old, (), aux, coef_x)
                 fields, _f = compute(0, values, None)
                 t_ay[0, rows, :] = fields[0]
                 t_ay[1, rows, :] = fields[2]
@@ -435,8 +450,8 @@
                     flat_h[across(0, i + 1, SUB - 1), :] = r_ay[s, 0, rows, :] - half * e2
                     flat_h[across(2, i + 1, SUB - 1), :] = r_ay[s, 1, rows, :] + half * e0
 
-        def fix_x(s):
-            @pl.when(has_ly)
+        def fix_high(s):
+            @pl.when(both(has_hx, has_ly))
             def _():
                 edge = pl.ds(SUB - 1, 1)
                 H[2, rows_x, edge, :] = (
@@ -448,56 +463,94 @@
                 H[1, rows_x, inner, :] = H[1, rows_x, inner, :] + half * r_ex[s, 1]
                 H[2, rows_x, inner, :] = H[2, rows_x, inner, :] - half * r_ex[s, 0]
 
+        def fix_low(s):
             @pl.when(has_lx)
             def _():
                 H[1, 0, inner, :] = r_ax[s, 0] + half * E[2, 0, own, :]
                 H[2, 0, inner, :] = r_ax[s, 1] - half * E[1, 0, own, :]
+
+            @pl.when(both(has_lx, has_hy))
+            def _():
                 edge = pl.ds(SUB + right, 1)
                 H[2, 0, edge, :] = H[2, 0, edge, :] + half * r_c0[s, pl.ds(0, 1), :]
 
+        odd = lax.rem(gx, 2) == 1
+
+        def in_turn(high, low):
+            @pl.when(odd)
+            def _():
+                high()
+                low()
+
+            @pl.when(jnp.logical_not(odd))
+            def _():
+                low()
+                high()
+
+        count = groups * tiles
         edge_x[pl.ds(rows_y, SUB), :] = zero
         edge_y[pl.ds(rows_x, SUB), :] = zero
-        count = groups * tiles
-        sweep(0, count)
+        fields_in[0].wait()
+        fields_in[1].wait()
+        wait_slots(0)
+        partial_high([[E[c, top, pl.ds(t * SUB, SUB), :] for c in range(3)] for t in range(tiles)])
         t_ex[0] = E[1, 0, own, :]
         t_ex[1] = E[2, 0, own, :]
-        t_ax[0] = H[1, rows_x, inner, :]
-        t_ax[1] = H[2, rows_x, inner, :]
-        t_c0[...] = E[0, top, pl.ds(0, SUB), :]
         t_c1[...] = E[1, 0, pl.ds(rows_y - SUB, SUB), :]
+        partial_y([[flat_e[across(c, u * SUB, right), :] for c in range(3)] for u in range(packs)])
         for u in range(packs):
             i = u * SUB
             rows = pl.ds(i, SUB)
             t_ey[0, rows, :] = flat_e[across(0, i, 0), :]
             t_ey[1, rows, :] = flat_e[across(2, i, 0), :]
-            t_ay[0, rows, :] = flat_h[across(0, i + 1, SUB + right), :]
-            t_ay[1, rows, :] = flat_h[across(2, i + 1, SUB + right), :]
-        first_x, first_y = exchange(0)
-        start(first_x)
+        pl.semaphore_wait(barrier, sum(jnp.where(present, 1, 0) for present, _t in links))
+        first_high, first_low, first_y = exchange(0)
+        in_turn(lambda: start(first_high), lambda: start(first_low))
         start(first_y)
+        sweep(0, count)
+        fields_in[2].wait()
+        materials()
+        wait_slots(1)
 
         def advance(step, carry):
             s = lax.rem(step, 2)
-            old_x, old_y = exchange(s)
-            new_x, new_y = exchange(1 - s)
-            more = step < STEPS - 1
-            finish(old_y)
+            out_high, out_low, old_y = exchange(s)
+            new_high, new_low, new_y = exchange(1 - s)
+            arrived(old_y)
             fix_y(s)
-            finish(old_x)
-            fix_x(s)
-
-            @pl.when(more)
-            def _():
-                faces_x()
-                start(new_x)
-                faces_y()
-                start(new_y)
-
+            left(old_y)
+            left(out_high)
+            left(out_low)
+
+            def high():
+                arrived(out_low)
+                fix_high(s)
+                face_high()
+                start(new_high)
+
+            def low():
+                arrived(out_high)
+                fix_low(s)
+                face_low()
+                start(new_low)
+
+            in_turn(high, low)
+            faces_y()
+            start(new_y)
             sweep(1, count)
-            sweep(0, jnp.where(more, count, 0))
+            sweep(0, count)
             return carry
 
-        lax.fori_loop(0, STEPS, advance, 0)
+        lax.fori_loop(0, STEPS - 1, advance, 0)
+        s = (STEPS - 1) % 2
+        last_high, last_low, last_y = exchange(s)
+        for moves in (last_y, last_low, last_high):
+            arrived(moves)
+            left(moves)
+        fix_y(s)
+        fix_high(s)
+        fix_low(s)
+        sweep(1, count)
 
     return kernel
 
@@ -555,7 +608,7 @@
             + [pltpu.VMEM(f, f32) for f in faces]
             + [pltpu.VMEM((2,) + f, f32) for f in faces]
             + [
-                pltpu.SemaphoreType.DMA((11,)),
+                pltpu.SemaphoreType.DMA((17,)),
                 pltpu.SemaphoreType.DMA((6,)),
                 pltpu.SemaphoreType.DMA((6, 2)),
             ],

time: 74.7 us -> 68.9 us (0.922)
  Pallas kernels: 73.9 us -> 68.1 us
    pallas_call x1, Pallas kernels: 70.2 us -> 64.3 us  [shards(): pl.pallas_call(make_kernel(size_x, size_y, rows_x, rows_y, depth_z), out_...]
where the time goes in v2:
time: 68.9 us; the launch traced here: 68.7 us
  Pallas kernels  68.1 us (99%)
    pallas_call x1, Pallas kernels, shards(): pl.pallas_call(make_kernel(size_x, size_y, rows_x, rows_y, depth_z), out_...  64.3 us
    pallas_call x1, Pallas kernels, shards(): pl.pallas_call(make_writer(rows_x, rows_y), out_shape=[jax.ShapeDtypeStru...  3.77 us

profile of v2, /device:TPU:0, one launch (start us, length us, event | category | flops | bytes accessed | tf_op | source)
XLA Modules:
  0.0 68.7 jit_solution(12159757442410897018)
XLA Ops:
  0.6 64.3 %shard_map.85 = (f32[3,33,40,128]{3,2,1,0:T(8,128)S(1)}, f32[3,33,40,128]{3,2,1,0:T(8,128)S(1)}, f32[12,32,32,128]{3,2,1,0:T(8,128)S(1)}) custom-call(f32[3,32,32,128]{3,2,1,0:T(8,128)} %e_in.1, f32[3,32,32,128]{3,2,1,0:T(8,128)} %h_in.1, f32[12,32,32,128]{3,2,1,0:T(8,128)} %p_in.1, s32[32,32,128]{2,1,0:T(8,128)} %m_in.1, f32[8]{0:T(128)} %eps_ref.1, f32[8]{0:T(128)} %sig_ref.1), custom_call_target="tpu_custom_call" | custom-call | tf_op jit(solution)/shard_map/pallas_call | solution.py:593
  65.0 3.8 %shard_map.86 = (f32[3,32,32,128]{3,2,1,0:T(8,128)}, f32[3,32,32,128]{3,2,1,0:T(8,128)}, f32[12,32,32,128]{3,2,1,0:T(8,128)}) custom-call(f32[3,33,40,128]{3,2,1,0:T(8,128)S(1)} %get-tuple-element.6.E, f32[3,33,40,128]{3,2,1,0:T(8,128)S(1)} %get-tuple-element.7.H, f32[12,32,32,128]{3,2,1,0:T(8,128)S(1)} %get-tuple-element.8.S), custom_call_target="tpu_custom_call" | custom-call | tf_op jit(solution)/shard_map/pallas_call | solution.py:619

commit v3 on v2

--- a/solution.py
+++ b/solution.py
@@ -295,9 +295,11 @@
             diag_c0, diag_c1 = both(has_hx, has_ly), both(has_lx, has_hy)
             moves = (
                 (diag_c0, (hx, ly), diag_c1, t_c0.at[one], r_c0.at[s, one]),
-                (has_hx, (hx, gy), has_lx, t_ax, r_ax.at[s]),
+                (has_hx, (hx, gy), has_lx, t_ax.at[1], r_ax.at[s, 1]),
+                (has_hx, (hx, gy), has_lx, t_ax.at[0], r_ax.at[s, 0]),
                 (diag_c1, (lx, hy), diag_c0, t_c1.at[last], r_c1.at[s, last]),
-                (has_lx, (lx, gy), has_hx, t_ex, r_ex.at[s]),
+                (has_lx, (lx, gy), has_hx, t_ex.at[0], r_ex.at[s, 0]),
+                (has_lx, (lx, gy), has_hx, t_ex.at[1], r_ex.at[s, 1]),
                 (has_ly, (gx, ly), has_hy, t_ey, r_ey.at[s]),
                 (has_hy, (gx, hy), has_ly, t_ay, r_ay.at[s]),
             )
@@ -316,7 +318,7 @@
                 )
                 for n, (sends, target, gets, src, dst) in enumerate(moves)
             ]
-            return made[:2], made[2:4], made[4:]
+            return made[:3], made[3:6], made[6:]
 
         own = pl.ds(0, rows_y)
         inner = pl.ds(SUB, rows_y)
@@ -359,13 +361,12 @@
         def coefs_y(k, y):
             return [cy[k, n, pl.ds(y, SUB), :] for n in range(3)]
 
-        def face_low():
+        def face_low(c):
             for t in range(tiles):
                 y = t * SUB
                 fields, _f = compute(1, loads(1, 0, y, False, True), coefs_y(1, y))
-                t_ex[0, pl.ds(y, SUB), :] = fields[1]
-                t_ex[1, pl.ds(y, SUB), :] = fields[2]
-                if t == tiles - 1:
+                t_ex[c - 1, pl.ds(y, SUB), :] = fields[c]
+                if c == 1 and t == tiles - 1:
                     t_c1[...] = fields[1]
 
         def face_high():
@@ -373,22 +374,24 @@
             for t in range(tiles):
                 y = t * SUB
                 fields.append(compute(1, loads(1, top, y, False, True), coefs_y(1, y))[0])
-            partial_high(fields)
-
-        def partial_high(e_new):
-            t_c0[...] = e_new[0][0]
+            t_c0[...] = fields[0][0]
             for t in range(tiles):
-                edge_x[pl.ds(t * SUB, SUB), :] = e_new[t][0]
+                rows = pl.ds(t * SUB, SUB)
+                edge_x[0, rows, :] = fields[t][0]
+                edge_x[1, rows, :] = fields[t][1]
+                edge_x[2, rows, :] = fields[t][2]
+
+        def partial_high(c):
             for t in range(tiles):
                 y = t * SUB
                 rows, at = pl.ds(y, SUB), pl.ds(y + SUB, SUB)
-                old = [H[c, rows_x, at, :] for c in range(3)]
+                e_new = [edge_x[n, rows, :] for n in range(3)]
+                old = [H[n, rows_x, at, :] for n in range(3)]
                 aux = {n: S[n, top, rows, :] for n in (1, 2, 0, 5)}
-                side_y = (edge_x[pl.ds(y + 1, SUB), :], zero)
-                values = (e_new[t], (zero, zero), side_y, old, (), aux, None)
+                side_y = (edge_x[0, pl.ds(y + 1, SUB), :], zero)
+                values = (e_new, (zero, zero), side_y, old, (), aux, None)
                 fields, _f = compute(0, values, coefs_y(0, y))
-                t_ax[0, rows, :] = fields[1]
-                t_ax[1, rows, :] = fields[2]
+                t_ax[c - 1, rows, :] = fields[c]
 
         def packed_e(r, u):
             i = u * SUB
@@ -463,10 +466,9 @@
                 H[1, rows_x, inner, :] = H[1, rows_x, inner, :] + half * r_ex[s, 1]
                 H[2, rows_x, inner, :] = H[2, rows_x, inner, :] - half * r_ex[s, 0]
 
-        def fix_low(s):
+        def fix_low_2(s):
             @pl.when(has_lx)
             def _():
-                H[1, 0, inner, :] = r_ax[s, 0] + half * E[2, 0, own, :]
                 H[2, 0, inner, :] = r_ax[s, 1] - half * E[1, 0, own, :]
 
             @pl.when(both(has_lx, has_hy))
@@ -474,6 +476,11 @@
                 edge = pl.ds(SUB + right, 1)
                 H[2, 0, edge, :] = H[2, 0, edge, :] + half * r_c0[s, pl.ds(0, 1), :]
 
+        def fix_low_1(s):
+            @pl.when(has_lx)
+            def _():
+                H[1, 0, inner, :] = r_ax[s, 0] + half * E[2, 0, own, :]
+
         odd = lax.rem(gx, 2) == 1
 
         def in_turn(high, low):
@@ -488,12 +495,16 @@
                 high()
 
         count = groups * tiles
-        edge_x[pl.ds(rows_y, SUB), :] = zero
+        edge_x[0, pl.ds(rows_y, SUB), :] = zero
         edge_y[pl.ds(rows_x, SUB), :] = zero
         fields_in[0].wait()
         fields_in[1].wait()
         wait_slots(0)
-        partial_high([[E[c, top, pl.ds(t * SUB, SUB), :] for c in range(3)] for t in range(tiles)])
+        t_c0[...] = E[0, top, pl.ds(0, SUB), :]
+        for c in range(3):
+            edge_x[c, own, :] = E[c, top, own, :]
+        partial_high(2)
+        partial_high(1)
         t_ex[0] = E[1, 0, own, :]
         t_ex[1] = E[2, 0, own, :]
         t_c1[...] = E[1, 0, pl.ds(rows_y - SUB, SUB), :]
@@ -526,13 +537,20 @@
                 arrived(out_low)
                 fix_high(s)
                 face_high()
-                start(new_high)
+                partial_high(2)
+                start(new_high[:2])
+                partial_high(1)
+                start(new_high[2:])
 
             def low():
-                arrived(out_high)
-                fix_low(s)
-                face_low()
-                start(new_low)
+                arrived(out_high[:2])
+                fix_low_2(s)
+                face_low(1)
+                start(new_low[:2])
+                arrived(out_high[2:])
+                fix_low_1(s)
+                face_low(2)
+                start(new_low[2:])
 
             in_turn(high, low)
             faces_y()
@@ -549,7 +567,8 @@
             left(moves)
         fix_y(s)
         fix_high(s)
-        fix_low(s)
+        fix_low_2(s)
+        fix_low_1(s)
         sweep(1, count)
 
     return kernel
@@ -602,15 +621,15 @@
                 pltpu.VMEM((2, 3, rows_x, SUB, depth_z), f32),
                 pltpu.VMEM((2, 3, rows_y, depth_z), f32),
                 pltpu.VMEM((2, 3, rows_x, depth_z), f32),
-                pltpu.VMEM((rows_y + SUB, depth_z), f32),
+                pltpu.VMEM((3, rows_y + SUB, depth_z), f32),
                 pltpu.VMEM((rows_x + SUB, depth_z), f32),
             ]
             + [pltpu.VMEM(f, f32) for f in faces]
             + [pltpu.VMEM((2,) + f, f32) for f in faces]
             + [
                 pltpu.SemaphoreType.DMA((17,)),
-                pltpu.SemaphoreType.DMA((6,)),
-                pltpu.SemaphoreType.DMA((6, 2)),
+                pltpu.SemaphoreType.DMA((8,)),
+                pltpu.SemaphoreType.DMA((8, 2)),
             ],
             compiler_params=pltpu.CompilerParams(
                 collective_id=0, has_side_effects=True, vmem_limit_bytes=53 << 20

time: 68.9 us -> 67.9 us (0.985)
  Pallas kernels: 68.1 us -> 67.1 us
    pallas_call x1, Pallas kernels: 64.3 us -> 63.3 us  [shards(): pl.pallas_call(make_kernel(size_x, size_y, rows_x, rows_y, depth_z), out_...]
where the time goes in v3:
time: 67.9 us; the launch traced here: 67.7 us
  Pallas kernels  67.1 us (99%)
    pallas_call x1, Pallas kernels, shards(): pl.pallas_call(make_kernel(size_x, size_y, rows_x, rows_y, depth_z), out_...  63.3 us
    pallas_call x1, Pallas kernels, shards(): pl.pallas_call(make_writer(rows_x, rows_y), out_shape=[jax.ShapeDtypeStru...  3.77 us

profile of v3, /device:TPU:0, one launch (start us, length us, event | category | flops | bytes accessed | tf_op | source)
XLA Modules:
  0.0 67.7 jit_solution(7401793973933880292)
XLA Ops:
  0.6 63.3 %shard_map.85 = (f32[3,33,40,128]{3,2,1,0:T(8,128)S(1)}, f32[3,33,40,128]{3,2,1,0:T(8,128)S(1)}, f32[12,32,32,128]{3,2,1,0:T(8,128)S(1)}) custom-call(f32[3,32,32,128]{3,2,1,0:T(8,128)} %e_in.1, f32[3,32,32,128]{3,2,1,0:T(8,128)} %h_in.1, f32[12,32,32,128]{3,2,1,0:T(8,128)} %p_in.1, s32[32,32,128]{2,1,0:T(8,128)} %m_in.1, f32[8]{0:T(128)} %eps_ref.1, f32[8]{0:T(128)} %sig_ref.1), custom_call_target="tpu_custom_call" | custom-call | tf_op jit(solution)/shard_map/pallas_call | solution.py:612
  63.9 3.8 %shard_map.86 = (f32[3,32,32,128]{3,2,1,0:T(8,128)}, f32[3,32,32,128]{3,2,1,0:T(8,128)}, f32[12,32,32,128]{3,2,1,0:T(8,128)}) custom-call(f32[3,33,40,128]{3,2,1,0:T(8,128)S(1)} %get-tuple-element.6.E, f32[3,33,40,128]{3,2,1,0:T(8,128)S(1)} %get-tuple-element.7.H, f32[12,32,32,128]{3,2,1,0:T(8,128)S(1)} %get-tuple-element.8.S), custom_call_target="tpu_custom_call" | custom-call | tf_op jit(solution)/shard_map/pallas_call | solution.py:638

commit v4 on v3

--- a/solution.py
+++ b/solution.py
@@ -44,6 +44,98 @@
     )
 
 
+def make_cell(
+    E, H, S, keep, drive, cx, cy, zc, slab_x, slab_y, tiles, depth_z, e_to, s_to, s_base
+):
+    lane = lax.broadcasted_iota(jnp.int32, (SUB, depth_z), 1)
+    not_last = lane < depth_z - 1
+    not_first = lane > 0
+
+    def term(old, d, coef):
+        b, a, q = coef
+        renewed = b * old + a * d
+        return q * d + renewed, renewed
+
+    def loads(k, i, y, in_x, in_y):
+        rows, at = pl.ds(y, SUB), pl.ds(y + SUB, SUB)
+        first = 6 * k
+        if k == 0:
+            src, j, now, step, line = E, i, rows, 1, pl.ds(y + 1, SUB)
+            old = [H[c, i + 1, at, :] for c in range(3)]
+            mats = ()
+        else:
+            src, j, now, step, line = H, i + 1, at, -1, pl.ds(y + SUB - 1, SUB)
+            old = [E[c, i, rows, :] for c in range(3)]
+            mats = (keep[i, rows, :], drive[i, rows, :])
+        own = [src[c, j, now, :] for c in range(3)]
+        side_x = [src[c, j + step, now, :] for c in (1, 2)]
+        side_y = [src[c, j, line, :] for c in (0, 2)]
+        slots = [1, 2] + ([3, 4] if in_x else []) + ([0, 5] if in_y else [])
+        aux = {n: S[first + n, i, rows, :] for n in slots}
+        coef_x = [cx[k, n, i] for n in range(3)] if in_x else None
+        return own, side_x, side_y, old, mats, aux, coef_x
+
+    def compute(k, values, coef_y):
+        own, (x1, x2), (y0, y2), old, mats, aux, coef_x = values
+        f0, f1, f2 = own
+        if k == 0:
+            dx1, dx2, dy0, dy2 = x1 - f1, x2 - f2, y0 - f0, y2 - f2
+            dz0 = jnp.where(not_last, pltpu.roll(f0, depth_z - 1, 1), 0.0) - f0
+            dz1 = jnp.where(not_last, pltpu.roll(f1, depth_z - 1, 1), 0.0) - f1
+        else:
+            dx1, dx2, dy0, dy2 = f1 - x1, f2 - x2, f0 - y0, f2 - y2
+            dz0 = f0 - jnp.where(not_first, pltpu.roll(f0, 1, 1), 0.0)
+            dz1 = f1 - jnp.where(not_first, pltpu.roll(f1, 1, 1), 0.0)
+        fresh = {}
+        dz1, fresh[1] = term(aux[1], dz1, zc[k])
+        dz0, fresh[2] = term(aux[2], dz0, zc[k])
+        if coef_x is not None:
+            dx2, fresh[3] = term(aux[3], dx2, coef_x)
+            dx1, fresh[4] = term(aux[4], dx1, coef_x)
+        if coef_y is not None:
+            dy2, fresh[0] = term(aux[0], dy2, coef_y)
+            dy0, fresh[5] = term(aux[5], dy0, coef_y)
+        curls = (dy2 - dz1, dz0 - dx2, dx1 - dy0)
+        if k == 0:
+            return [o - time_step * c for o, c in zip(old, curls)], fresh
+        return [mats[0] * o + mats[1] * c for o, c in zip(old, curls)], fresh
+
+    def stores(k, i, y, result):
+        fields, fresh = result
+        for c in range(3):
+            if k == 0:
+                H[c, i + 1, pl.ds(y + SUB, SUB), :] = fields[c]
+            else:
+                e_to[c, i, pl.ds(y, SUB), :] = fields[c]
+        for n, v in fresh.items():
+            s_to[6 * k + n - s_base, i, pl.ds(y, SUB), :] = v
+
+    def run(k, i0, y, in_x, in_y):
+        coef_y = [cy[k, n, pl.ds(y, SUB), :] for n in range(3)] if in_y else None
+        ready = [loads(k, i0 + u, y, in_x, in_y) for u in range(AHEAD)]
+        for u in range(GROUP):
+            if u + AHEAD < GROUP:
+                ready.append(loads(k, i0 + u + AHEAD, y, in_x, in_y))
+            stores(k, i0 + u, y, compute(k, ready[u], coef_y))
+
+    def unit(k, g, t):
+        low_x, low_y = g * GROUP < PML, t * SUB < PML
+        px = jnp.where(low_x, slab_x[0], slab_x[1])
+        py = jnp.where(low_y, slab_y[0], slab_y[1])
+        i0, y = g * GROUP, pl.multiple_of(t * SUB, SUB)
+
+        def split_y(in_x):
+            lax.cond(
+                py,
+                lambda: run(k, i0, y, in_x, True),
+                lambda: run(k, i0, y, in_x, False),
+            )
+
+        lax.cond(px, lambda: split_y(True), lambda: split_y(False))
+
+    return loads, compute, unit
+
+
 def make_kernel(size_x, size_y, rows_x, rows_y, depth_z):
     groups = rows_x // GROUP
     tiles = rows_y // SUB
@@ -51,7 +143,7 @@
 
     def kernel(
         e_in, h_in, p_in, m_in, eps_ref, sig_ref, E, H, S,
-        keep, drive, mat, cx, cy, cp, edge_x, edge_y,
+        keep, drive, cx, cy, mat, cp, edge_x, edge_y,
         t_ex, t_ey, t_ax, t_ay, t_c0, t_c1,
         r_ex, r_ey, r_ax, r_ay, r_c0, r_c1,
         in_sem, send_sem, recv_sem,
@@ -72,66 +164,83 @@
             (both(has_lx, has_hy), (lx, hy)),
         )
 
-        def field_copies():
-            pairs = (
-                (e_in, E.at[:, pl.ds(0, rows_x), pl.ds(0, rows_y), :]),
-                (h_in, H.at[:, pl.ds(1, rows_x), pl.ds(SUB, rows_y), :]),
-                (m_in, mat),
+        mid = pl.ds(0, rows_y)
+
+        def e_copy(first, number, n):
+            layers = pl.ds(first, number)
+            return pltpu.make_async_copy(e_in.at[:, layers], E.at[:, layers, mid, :], in_sem.at[n])
+
+        def h_copy(first, number, n):
+            return pltpu.make_async_copy(
+                h_in.at[:, pl.ds(first, number)],
+                H.at[:, pl.ds(first + 1, number), pl.ds(SUB, rows_y), :],
+                in_sem.at[n],
             )
-            return [pltpu.make_async_copy(a, b, in_sem.at[n]) for n, (a, b) in enumerate(pairs)]
-
-        def slot_copies(k):
-            first, base = 6 * k, 3 + 7 * k
-            pair = pl.ds(first + 1, 2)
-            always = pltpu.make_async_copy(p_in.at[pair], S.at[pair], in_sem.at[base])
-            guarded = []
+
+        def slot_copies(k, first, number, n):
+            layers, pair = pl.ds(first, number), pl.ds(6 * k + 1, 2)
+            made = [
+                (
+                    None,
+                    pltpu.make_async_copy(
+                        p_in.at[pair, layers], S.at[pair, layers], in_sem.at[n]
+                    ),
+                )
+            ]
             for side in (0, 1):
-                half_x, pair = pl.ds(side * PML, PML), pl.ds(first + 3, 2)
-                guarded.append(
+                rows = pl.ds(side * PML, PML)
+                for j, slot in enumerate((6 * k, 6 * k + 5)):
+                    made.append(
+                        (
+                            slab_y[side],
+                            pltpu.make_async_copy(
+                                p_in.at[slot, layers, rows],
+                                S.at[slot, layers, rows],
+                                in_sem.at[n + 1 + 2 * side + j],
+                            ),
+                        )
+                    )
+            return made
+
+        def across_copies(k, n):
+            pair = pl.ds(6 * k + 3, 2)
+            made = []
+            for side in (0, 1):
+                layers = pl.ds(side * PML, PML)
+                made.append(
                     (
                         slab_x[side],
                         pltpu.make_async_copy(
-                            p_in.at[pair, half_x], S.at[pair, half_x], in_sem.at[base + 1 + side]
+                            p_in.at[pair, layers], S.at[pair, layers], in_sem.at[n + side]
                         ),
                     )
                 )
-                for n, slot in enumerate((first, first + 5)):
-                    guarded.append(
-                        (
-                            slab_y[side],
-                            pltpu.make_async_copy(
-                                p_in.at[slot, :, half_x],
-                                S.at[slot, :, half_x],
-                                in_sem.at[base + 3 + 2 * side + n],
-                            ),
-                        )
-                    )
-            return always, guarded
-
-        def start_slots(k):
-            always, guarded = slot_copies(k)
-            always.start()
-            for present, copy in guarded:
-
-                @pl.when(present)
-                def _():
-                    copy.start()
-
-        def wait_slots(k):
-            always, guarded = slot_copies(k)
-            always.wait()
-            for present, copy in guarded:
-
-                @pl.when(present)
-                def _():
-                    copy.wait()
-
-        fields_in = field_copies()
-        fields_in[0].start()
-        fields_in[1].start()
-        start_slots(0)
-        fields_in[2].start()
-        start_slots(1)
+            return made
+
+        def each(copies, act):
+            for present, copy in copies:
+                if present is None:
+                    act(copy)
+                else:
+
+                    @pl.when(present)
+                    def _():
+                        act(copy)
+
+        def begin(copies):
+            each(copies, lambda copy: copy.start())
+
+        def settle(copies):
+            each(copies, lambda copy: copy.wait())
+
+        rim = [(None, e_copy(top, 1, 0)), (None, h_copy(top, 1, 1))]
+        rim += slot_copies(0, top, 1, 2) + [(None, e_copy(0, 1, 7))]
+        rest = [(None, e_copy(1, top - 1, 8)), (None, h_copy(0, top, 9))]
+        rest += slot_copies(0, 0, top, 10) + across_copies(0, 15)
+        kinds = [(None, pltpu.make_async_copy(m_in, mat, in_sem.at[17]))]
+        later = slot_copies(1, 0, rows_x, 18) + across_copies(1, 23)
+        for copies in (rim, rest, kinds, later):
+            begin(copies)
 
         barrier = pltpu.get_barrier_semaphore()
         for present, target in links:
@@ -142,13 +251,6 @@
 
         zero = jnp.zeros((SUB, depth_z), jnp.float32)
         for side in (0, 1):
-
-            @pl.when(jnp.logical_not(slab_x[side]))
-            def _():
-                @pl.loop(side * PML, side * PML + PML)
-                def _(i):
-                    for s in (3, 4, 9, 10):
-                        S[s, i] = jnp.zeros((rows_y, depth_z), jnp.float32)
 
             @pl.when(jnp.logical_not(slab_y[side]))
             def _():
@@ -159,32 +261,42 @@
                             (PML, depth_z), jnp.float32
                         )
 
-        for c in range(3):
-            for t in range(tiles):
-                E[c, rows_x, pl.ds(t * SUB, SUB), :] = zero
-                H[c, 0, pl.ds(SUB + t * SUB, SUB), :] = zero
-
-        @pl.loop(0, rows_x)
-        def _(i):
-            for c in range(3):
-                E[c, i, pl.ds(rows_y, SUB), :] = zero
-                H[c, i + 1, pl.ds(0, SUB), :] = zero
-
         lane = lax.broadcasted_iota(jnp.int32, (SUB, depth_z), 1)
         row = lax.broadcasted_iota(jnp.int32, (rows_y, depth_z), 0)
-        column = lax.broadcasted_iota(jnp.int32, (rows_x, depth_z), 0)
-        plane = lax.broadcasted_iota(jnp.int32, (rows_x, SUB, depth_z), 0)
         zc = []
         for k, shift in enumerate((0.5, 0.0)):
             zc.append(profile(lane, depth_z, shift))
             for n, v in enumerate(profile(row + gy * rows_y, size_y * rows_y, shift)):
                 cy[k, n] = v
-            for n, v in enumerate(profile(plane + gx * rows_x, size_x * rows_x, shift)):
-                cx[k, n] = v
-            for n, v in enumerate(profile(column + gx * rows_x, size_x * rows_x, shift)):
-                cp[k, n] = v
-        not_last = lane < depth_z - 1
-        not_first = lane > 0
+
+        def clear_rest():
+            for side in (0, 1):
+
+                @pl.when(jnp.logical_not(slab_x[side]))
+                def _():
+                    @pl.loop(side * PML, side * PML + PML)
+                    def _(i):
+                        for s in (3, 4, 9, 10):
+                            S[s, i] = jnp.zeros((rows_y, depth_z), jnp.float32)
+
+            for c in range(3):
+                for t in range(tiles):
+                    E[c, rows_x, pl.ds(t * SUB, SUB), :] = zero
+                    H[c, 0, pl.ds(SUB + t * SUB, SUB), :] = zero
+
+            @pl.loop(0, rows_x)
+            def _(i):
+                for c in range(3):
+                    E[c, i, pl.ds(rows_y, SUB), :] = zero
+                    H[c, i + 1, pl.ds(0, SUB), :] = zero
+
+            column = lax.broadcasted_iota(jnp.int32, (rows_x, depth_z), 0)
+            plane = lax.broadcasted_iota(jnp.int32, (rows_x, SUB, depth_z), 0)
+            for k, shift in enumerate((0.5, 0.0)):
+                for n, v in enumerate(profile(plane + gx * rows_x, size_x * rows_x, shift)):
+                    cx[k, n] = v
+                for n, v in enumerate(profile(column + gx * rows_x, size_x * rows_x, shift)):
+                    cp[k, n] = v
 
         def materials():
             keep_vals, drive_vals = [], []
@@ -208,87 +320,9 @@
                     keep[i, rows, :] = kv
                     drive[i, rows, :] = dv
 
-        def term(old, d, coef):
-            b, a, q = coef
-            renewed = b * old + a * d
-            return q * d + renewed, renewed
-
-        def loads(k, i, y, in_x, in_y):
-            rows, at = pl.ds(y, SUB), pl.ds(y + SUB, SUB)
-            first = 6 * k
-            if k == 0:
-                src, j, now, step, line = E, i, rows, 1, pl.ds(y + 1, SUB)
-                old = [H[c, i + 1, at, :] for c in range(3)]
-                mats = ()
-            else:
-                src, j, now, step, line = H, i + 1, at, -1, pl.ds(y + SUB - 1, SUB)
-                old = [E[c, i, rows, :] for c in range(3)]
-                mats = (keep[i, rows, :], drive[i, rows, :])
-            own = [src[c, j, now, :] for c in range(3)]
-            side_x = [src[c, j + step, now, :] for c in (1, 2)]
-            side_y = [src[c, j, line, :] for c in (0, 2)]
-            slots = [1, 2] + ([3, 4] if in_x else []) + ([0, 5] if in_y else [])
-            aux = {n: S[first + n, i, rows, :] for n in slots}
-            coef_x = [cx[k, n, i] for n in range(3)] if in_x else None
-            return own, side_x, side_y, old, mats, aux, coef_x
-
-        def compute(k, values, coef_y):
-            own, (x1, x2), (y0, y2), old, mats, aux, coef_x = values
-            f0, f1, f2 = own
-            if k == 0:
-                dx1, dx2, dy0, dy2 = x1 - f1, x2 - f2, y0 - f0, y2 - f2
-                dz0 = jnp.where(not_last, pltpu.roll(f0, depth_z - 1, 1), 0.0) - f0
-                dz1 = jnp.where(not_last, pltpu.roll(f1, depth_z - 1, 1), 0.0) - f1
-            else:
-                dx1, dx2, dy0, dy2 = f1 - x1, f2 - x2, f0 - y0, f2 - y2
-                dz0 = f0 - jnp.where(not_first, pltpu.roll(f0, 1, 1), 0.0)
-                dz1 = f1 - jnp.where(not_first, pltpu.roll(f1, 1, 1), 0.0)
-            fresh = {}
-            dz1, fresh[1] = term(aux[1], dz1, zc[k])
-            dz0, fresh[2] = term(aux[2], dz0, zc[k])
-            if coef_x is not None:
-                dx2, fresh[3] = term(aux[3], dx2, coef_x)
-                dx1, fresh[4] = term(aux[4], dx1, coef_x)
-            if coef_y is not None:
-                dy2, fresh[0] = term(aux[0], dy2, coef_y)
-                dy0, fresh[5] = term(aux[5], dy0, coef_y)
-            curls = (dy2 - dz1, dz0 - dx2, dx1 - dy0)
-            if k == 0:
-                return [o - time_step * c for o, c in zip(old, curls)], fresh
-            return [mats[0] * o + mats[1] * c for o, c in zip(old, curls)], fresh
-
-        def stores(k, i, y, result):
-            fields, fresh = result
-            for c in range(3):
-                if k == 0:
-                    H[c, i + 1, pl.ds(y + SUB, SUB), :] = fields[c]
-                else:
-                    E[c, i, pl.ds(y, SUB), :] = fields[c]
-            for n, v in fresh.items():
-                S[6 * k + n, i, pl.ds(y, SUB), :] = v
-
-        def run(k, i0, y, in_x, in_y):
-            coef_y = [cy[k, n, pl.ds(y, SUB), :] for n in range(3)] if in_y else None
-            ready = [loads(k, i0 + u, y, in_x, in_y) for u in range(AHEAD)]
-            for u in range(GROUP):
-                if u + AHEAD < GROUP:
-                    ready.append(loads(k, i0 + u + AHEAD, y, in_x, in_y))
-                stores(k, i0 + u, y, compute(k, ready[u], coef_y))
-
-        def unit(k, g, t):
-            low_x, low_y = g * GROUP < PML, t * SUB < PML
-            px = jnp.where(low_x, slab_x[0], slab_x[1])
-            py = jnp.where(low_y, slab_y[0], slab_y[1])
-            i0, y = g * GROUP, pl.multiple_of(t * SUB, SUB)
-
-            def split_y(in_x):
-                lax.cond(
-                    py,
-                    lambda: run(k, i0, y, in_x, True),
-                    lambda: run(k, i0, y, in_x, False),
-                )
-
-            lax.cond(px, lambda: split_y(True), lambda: split_y(False))
+        loads, compute, unit = make_cell(
+            E, H, S, keep, drive, cx, cy, zc, slab_x, slab_y, tiles, depth_z, E, S, 0
+        )
 
         def exchange(s):
             one, last = pl.ds(0, 1), pl.ds(SUB - 1, 1)
@@ -497,9 +531,7 @@
         count = groups * tiles
         edge_x[0, pl.ds(rows_y, SUB), :] = zero
         edge_y[pl.ds(rows_x, SUB), :] = zero
-        fields_in[0].wait()
-        fields_in[1].wait()
-        wait_slots(0)
+        settle(rim)
         t_c0[...] = E[0, top, pl.ds(0, SUB), :]
         for c in range(3):
             edge_x[c, own, :] = E[c, top, own, :]
@@ -508,20 +540,22 @@
         t_ex[0] = E[1, 0, own, :]
         t_ex[1] = E[2, 0, own, :]
         t_c1[...] = E[1, 0, pl.ds(rows_y - SUB, SUB), :]
+        pl.semaphore_wait(barrier, sum(jnp.where(present, 1, 0) for present, _t in links))
+        first_high, first_low, first_y = exchange(0)
+        in_turn(lambda: start(first_high), lambda: start(first_low))
+        clear_rest()
+        settle(rest)
         partial_y([[flat_e[across(c, u * SUB, right), :] for c in range(3)] for u in range(packs)])
         for u in range(packs):
             i = u * SUB
             rows = pl.ds(i, SUB)
             t_ey[0, rows, :] = flat_e[across(0, i, 0), :]
             t_ey[1, rows, :] = flat_e[across(2, i, 0), :]
-        pl.semaphore_wait(barrier, sum(jnp.where(present, 1, 0) for present, _t in links))
-        first_high, first_low, first_y = exchange(0)
-        in_turn(lambda: start(first_high), lambda: start(first_low))
         start(first_y)
         sweep(0, count)
-        fields_in[2].wait()
+        settle(kinds)
         materials()
-        wait_slots(1)
+        settle(later)
 
         def advance(step, carry):
             s = lax.rem(step, 2)
@@ -569,26 +603,75 @@
         fix_high(s)
         fix_low_2(s)
         fix_low_1(s)
-        sweep(1, count)
 
     return kernel
 
 
-def make_writer(rows_x, rows_y):
-    def writer(E, H, S, e_out, h_out, p_out, out_sem):
-        outs = [
-            pltpu.make_async_copy(
-                E.at[:, pl.ds(0, rows_x), pl.ds(0, rows_y), :], e_out, out_sem.at[0]
-            ),
-            pltpu.make_async_copy(
-                H.at[:, pl.ds(1, rows_x), pl.ds(SUB, rows_y), :], h_out, out_sem.at[1]
-            ),
-            pltpu.make_async_copy(S, p_out, out_sem.at[2]),
-        ]
-        for c in outs:
+def make_writer(size_x, size_y, rows_x, rows_y, depth_z):
+    groups = rows_x // GROUP
+    tiles = rows_y // SUB
+
+    def writer(E, H, S, keep, drive, cx, cy, e_out, h_out, p_out, e_new, s_new, out_sem):
+        gx, gy = lax.axis_index("gx"), lax.axis_index("gy")
+        slab_x = (gx == 0, gx == size_x - 1)
+        slab_y = (gy == 0, gy == size_y - 1)
+        copy = pltpu.make_async_copy
+        h_part = copy(H.at[:, pl.ds(1, rows_x), pl.ds(SUB, rows_y), :], h_out, out_sem.at[0])
+        p_part = copy(S.at[pl.ds(0, 6)], p_out.at[pl.ds(0, 6)], out_sem.at[1])
+        h_part.start()
+        p_part.start()
+        slabs = []
+        for side in (0, 1):
+            half, pair = pl.ds(side * PML, PML), pl.ds(9, 2)
+            to, sem = p_out.at[pair, half], out_sem.at[2 + side]
+            early = copy(S.at[pair, half], to, sem)
+            slabs.append((slab_x[side], early, copy(s_new.at[pl.ds(3, 2), half], to, sem)))
+            for j, slot in enumerate((6, 11)):
+                to, sem = p_out.at[slot, :, half], out_sem.at[4 + 2 * side + j]
+                early = copy(S.at[slot, :, half], to, sem)
+                slabs.append((slab_y[side], early, copy(s_new.at[slot - 6, :, half], to, sem)))
+        for inside, early, _late in slabs:
+
+            @pl.when(jnp.logical_not(inside))
+            def _():
+                early.start()
+
+        zc = [profile(lax.broadcasted_iota(jnp.int32, (SUB, depth_z), 1), depth_z, 0.0)] * 2
+        _loads, _compute, unit = make_cell(
+            E, H, S, keep, drive, cx, cy, zc, slab_x, slab_y, tiles, depth_z, e_new, s_new, 6
+        )
+        made = []
+        for g in range(groups):
+            layers, pair, one_two = pl.ds(g * GROUP, GROUP), pl.ds(7, 2), pl.ds(1, 2)
+            made.append(
+                [
+                    copy(e_new.at[:, layers], e_out.at[:, layers], out_sem.at[8 + 2 * g]),
+                    copy(s_new.at[one_two, layers], p_out.at[pair, layers], out_sem.at[9 + 2 * g]),
+                ]
+            )
+
+            @pl.loop(0, tiles)
+            def _(t):
+                unit(1, g, t)
+
+            if g > 0:
+                for c in made[g - 1]:
+                    c.start()
+        h_part.wait()
+        for c in made[-1]:
             c.start()
-        for c in outs:
-            c.wait()
+        for inside, _early, late in slabs:
+
+            @pl.when(inside)
+            def _():
+                late.start()
+
+        p_part.wait()
+        for _inside, early, _late in slabs:
+            early.wait()
+        for pieces in made:
+            for c in pieces:
+                c.wait()
 
     return writer
 
@@ -609,17 +692,16 @@
         padded = (3, rows_x + 1, rows_y + SUB, depth_z)
         cell = (rows_x, rows_y, depth_z)
         vmem = pl.BlockSpec(memory_space=pltpu.VMEM)
+        strip = (2, 3, rows_x, SUB, depth_z)
+        edge = (2, 3, rows_y, depth_z)
+        held = (padded, padded, psi.shape, cell, cell, strip, edge)
         state = pl.pallas_call(
             make_kernel(size_x, size_y, rows_x, rows_y, depth_z),
-            out_shape=[pltpu.VMEM(padded, f32), pltpu.VMEM(padded, f32), pltpu.VMEM(psi.shape, f32)],
+            out_shape=[pltpu.VMEM(shape, f32) for shape in held],
             in_specs=[any_space] * 4 + [smem] * 2,
-            out_specs=[vmem] * 3,
+            out_specs=[vmem] * len(held),
             scratch_shapes=[
-                pltpu.VMEM(cell, f32),
-                pltpu.VMEM(cell, f32),
                 pltpu.VMEM(cell, jnp.int32),
-                pltpu.VMEM((2, 3, rows_x, SUB, depth_z), f32),
-                pltpu.VMEM((2, 3, rows_y, depth_z), f32),
                 pltpu.VMEM((2, 3, rows_x, depth_z), f32),
                 pltpu.VMEM((3, rows_y + SUB, depth_z), f32),
                 pltpu.VMEM((rows_x + SUB, depth_z), f32),
@@ -627,21 +709,25 @@
             + [pltpu.VMEM(f, f32) for f in faces]
             + [pltpu.VMEM((2,) + f, f32) for f in faces]
             + [
-                pltpu.SemaphoreType.DMA((17,)),
+                pltpu.SemaphoreType.DMA((25,)),
                 pltpu.SemaphoreType.DMA((8,)),
                 pltpu.SemaphoreType.DMA((8, 2)),
             ],
             compiler_params=pltpu.CompilerParams(
-                collective_id=0, has_side_effects=True, vmem_limit_bytes=53 << 20
+                collective_id=0, has_side_effects=True, vmem_limit_bytes=48 << 20
             ),
         )(e_field, h_field, psi, material, eps_table, sigma_table)
         return pl.pallas_call(
-            make_writer(rows_x, rows_y),
+            make_writer(size_x, size_y, rows_x, rows_y, depth_z),
             out_shape=[jax.ShapeDtypeStruct(a.shape, f32) for a in (e_field, h_field, psi)],
-            in_specs=[vmem] * 3,
+            in_specs=[vmem] * len(held),
             out_specs=[any_space] * 3,
-            scratch_shapes=[pltpu.SemaphoreType.DMA((3,))],
-            compiler_params=pltpu.CompilerParams(vmem_limit_bytes=24 << 20),
+            scratch_shapes=[
+                pltpu.VMEM((3,) + cell, f32),
+                pltpu.VMEM((6,) + cell, f32),
+                pltpu.SemaphoreType.DMA((8 + 2 * (rows_x // GROUP),)),
+            ],
+            compiler_params=pltpu.CompilerParams(vmem_limit_bytes=32 << 20),
         )(*state)
 
     split = P(None, "gx", "gy", None)

time: 67.9 us -> 66 us (0.972)
  Pallas kernels: 67.1 us -> 65.2 us
    pallas_call x1, Pallas kernels: 63.3 us -> 61.5 us  [shards(): pl.pallas_call(make_kernel(size_x, size_y, rows_x, rows_y, depth_z), out_...]
where the time goes in v4:
time: 66 us; the launch traced here: 65.8 us
  Pallas kernels  65.2 us (99%)
    pallas_call x1, Pallas kernels, shards(): pl.pallas_call(make_kernel(size_x, size_y, rows_x, rows_y, depth_z), out_...  61.5 us
    pallas_call x1, Pallas kernels, shards(): pl.pallas_call(make_writer(size_x, size_y, rows_x, rows_y, depth_z), out_...  3.72 us

profile of v4, /device:TPU:0, one launch (start us, length us, event | category | flops | bytes accessed | tf_op | source)
XLA Modules:
  0.0 65.8 jit_solution(7323920542992009965)
XLA Ops:
  0.6 61.5 %shard_map.85 = (f32[3,33,40,128]{3,2,1,0:T(8,128)S(1)}, f32[3,33,40,128]{3,2,1,0:T(8,128)S(1)}, f32[12,32,32,128]{3,2,1,0:T(8,128)S(1)}, f32[32,32,128]{2,1,0:T...) custom-call(f32[3,32,32,128]{3,2,1,0:T(8,128)} %e_in.1, ...), custom_call_target="tpu_custom_call" | custom-call | tf_op jit(solution)/shard_map/pallas_call | solution.py:698
  62.1 3.7 %shard_map.86 = (f32[3,32,32,128]{3,2,1,0:T(8,128)}, f32[3,32,32,128]{3,2,1,0:T(8,128)}, f32[12,32,32,128]{3,2,1,0:T(8,128)}) custom-call(f32[3,33,40,128]{3,2,1,0:T(8,128)S(1)} %get-tuple-element.10.E, f32[3,33,40,128]{3,2,1,0:T(8,128)S(1)} %get-tuple-element.11.H, f32[12,32,32,128]{3,2,1,0:T(8,128)S(1)} %get-tuple-element.12.S, ...), custom_call_target="tpu_custom_call" | custom-call | tf_op jit(solution)/shard_map/pallas_call | solution.py:720

commit v5 on v4

--- a/solution.py
+++ b/solution.py
@@ -164,6 +164,13 @@
             (both(has_lx, has_hy), (lx, hy)),
         )
 
+        barrier = pltpu.get_barrier_semaphore()
+        for present, target in links:
+
+            @pl.when(present)
+            def _():
+                pl.semaphore_signal(barrier, inc=1, device_id=target, device_id_type=MESH)
+
         mid = pl.ds(0, rows_y)
 
         def e_copy(first, number, n):
@@ -241,13 +248,6 @@
         later = slot_copies(1, 0, rows_x, 18) + across_copies(1, 23)
         for copies in (rim, rest, kinds, later):
             begin(copies)
-
-        barrier = pltpu.get_barrier_semaphore()
-        for present, target in links:
-
-            @pl.when(present)
-            def _():
-                pl.semaphore_signal(barrier, inc=1, device_id=target, device_id_type=MESH)
 
         zero = jnp.zeros((SUB, depth_z), jnp.float32)
         for side in (0, 1):
@@ -487,46 +487,61 @@
                     flat_h[across(0, i + 1, SUB - 1), :] = r_ay[s, 0, rows, :] - half * e2
                     flat_h[across(2, i + 1, SUB - 1), :] = r_ay[s, 1, rows, :] + half * e0
 
+        def fix_corner_high(s):
+            edge = pl.ds(SUB - 1, 1)
+            H[2, rows_x, edge, :] = H[2, rows_x, edge, :] - half * r_c1[s, pl.ds(SUB - 1, 1), :]
+
         def fix_high(s):
-            @pl.when(both(has_hx, has_ly))
-            def _():
-                edge = pl.ds(SUB - 1, 1)
-                H[2, rows_x, edge, :] = (
-                    H[2, rows_x, edge, :] - half * r_c1[s, pl.ds(SUB - 1, 1), :]
-                )
-
-            @pl.when(has_hx)
-            def _():
-                H[1, rows_x, inner, :] = H[1, rows_x, inner, :] + half * r_ex[s, 1]
-                H[2, rows_x, inner, :] = H[2, rows_x, inner, :] - half * r_ex[s, 0]
+            H[1, rows_x, inner, :] = H[1, rows_x, inner, :] + half * r_ex[s, 1]
+            H[2, rows_x, inner, :] = H[2, rows_x, inner, :] - half * r_ex[s, 0]
 
         def fix_low_2(s):
-            @pl.when(has_lx)
-            def _():
-                H[2, 0, inner, :] = r_ax[s, 1] - half * E[1, 0, own, :]
-
-            @pl.when(both(has_lx, has_hy))
-            def _():
-                edge = pl.ds(SUB + right, 1)
-                H[2, 0, edge, :] = H[2, 0, edge, :] + half * r_c0[s, pl.ds(0, 1), :]
+            H[2, 0, inner, :] = r_ax[s, 1] - half * E[1, 0, own, :]
+
+        def fix_corner_low(s):
+            edge = pl.ds(SUB + right, 1)
+            H[2, 0, edge, :] = H[2, 0, edge, :] + half * r_c0[s, pl.ds(0, 1), :]
 
         def fix_low_1(s):
-            @pl.when(has_lx)
-            def _():
-                H[1, 0, inner, :] = r_ax[s, 0] + half * E[2, 0, own, :]
+            H[1, 0, inner, :] = r_ax[s, 0] + half * E[2, 0, own, :]
+
+        def when(present, act):
+            @pl.when(present)
+            def _():
+                act()
+
+        def arrive_high(s, came):
+            corner, first, second = [copy for _s, _g, copy in came]
+
+            @pl.when(has_ly)
+            def _():
+                corner.wait_recv()
+                fix_corner_high(s)
+
+            first.wait_recv()
+            second.wait_recv()
+            fix_high(s)
+
+        def arrive_low_2(s, came):
+            corner, first, _second = [copy for _s, _g, copy in came]
+            first.wait_recv()
+            fix_low_2(s)
+
+            @pl.when(has_hy)
+            def _():
+                corner.wait_recv()
+                fix_corner_low(s)
+
+        def arrive_low_1(s, came):
+            came[2][2].wait_recv()
+            fix_low_1(s)
 
         odd = lax.rem(gx, 2) == 1
 
         def in_turn(high, low):
-            @pl.when(odd)
-            def _():
-                high()
-                low()
-
-            @pl.when(jnp.logical_not(odd))
-            def _():
-                low()
-                high()
+            when(both(odd, has_hx), high)
+            when(has_lx, low)
+            when(both(jnp.logical_not(odd), has_hx), high)
 
         count = groups * tiles
         edge_x[0, pl.ds(rows_y, SUB), :] = zero
@@ -568,23 +583,24 @@
             left(out_low)
 
             def high():
-                arrived(out_low)
-                fix_high(s)
+                corner, first, second = [copy for _s, _g, copy in new_high]
+                arrive_high(s, out_low)
                 face_high()
                 partial_high(2)
-                start(new_high[:2])
+                when(has_ly, corner.start)
+                first.start()
                 partial_high(1)
-                start(new_high[2:])
+                second.start()
 
             def low():
-                arrived(out_high[:2])
-                fix_low_2(s)
+                corner, first, second = [copy for _s, _g, copy in new_low]
+                arrive_low_2(s, out_high)
                 face_low(1)
-                start(new_low[:2])
-                arrived(out_high[2:])
-                fix_low_1(s)
+                when(has_hy, corner.start)
+                first.start()
+                arrive_low_1(s, out_high)
                 face_low(2)
-                start(new_low[2:])
+                second.start()
 
             in_turn(high, low)
             faces_y()
@@ -596,13 +612,17 @@
         lax.fori_loop(0, STEPS - 1, advance, 0)
         s = (STEPS - 1) % 2
         last_high, last_low, last_y = exchange(s)
+        arrived(last_y)
+        fix_y(s)
+
+        def last_from_low():
+            arrive_low_2(s, last_high)
+            arrive_low_1(s, last_high)
+
+        when(has_hx, lambda: arrive_high(s, last_low))
+        when(has_lx, last_from_low)
         for moves in (last_y, last_low, last_high):
-            arrived(moves)
             left(moves)
-        fix_y(s)
-        fix_high(s)
-        fix_low_2(s)
-        fix_low_1(s)
 
     return kernel
 

time: 66 us -> 65.7 us (level)
  no operation moved by 1% of the time
where the time goes in v5:
time: 65.7 us; the launch traced here: 65.6 us
  Pallas kernels  64.9 us (99%)
    pallas_call x1, Pallas kernels, shards(): pl.pallas_call(make_kernel(size_x, size_y, rows_x, rows_y, depth_z), out_...  61.2 us
    pallas_call x1, Pallas kernels, shards(): pl.pallas_call(make_writer(size_x, size_y, rows_x, rows_y, depth_z), out_...  3.72 us

profile of v5, /device:TPU:0, one launch (start us, length us, event | category | flops | bytes accessed | tf_op | source)
XLA Modules:
  0.0 65.6 jit_solution(16221003054006891422)
XLA Ops:
  0.6 61.2 %shard_map.85 = (f32[3,33,40,128]{3,2,1,0:T(8,128)S(1)}, f32[3,33,40,128]{3,2,1,0:T(8,128)S(1)}, f32[12,32,32,128]{3,2,1,0:T(8,128)S(1)}, f32[32,32,128]{2,1,0:T...) custom-call(f32[3,32,32,128]{3,2,1,0:T(8,128)} %e_in.1, ...), custom_call_target="tpu_custom_call" | custom-call | tf_op jit(solution)/shard_map/pallas_call | solution.py:718
  61.9 3.7 %shard_map.86 = (f32[3,32,32,128]{3,2,1,0:T(8,128)}, f32[3,32,32,128]{3,2,1,0:T(8,128)}, f32[12,32,32,128]{3,2,1,0:T(8,128)}) custom-call(f32[3,33,40,128]{3,2,1,0:T(8,128)S(1)} %get-tuple-element.10.E, f32[3,33,40,128]{3,2,1,0:T(8,128)S(1)} %get-tuple-element.11.H, f32[12,32,32,128]{3,2,1,0:T(8,128)S(1)} %get-tuple-element.12.S, ...), custom_call_target="tpu_custom_call" | custom-call | tf_op jit(solution)/shard_map/pallas_call | solution.py:740

commit v6 on v5

--- a/solution.py
+++ b/solution.py
@@ -143,7 +143,7 @@
 
     def kernel(
         e_in, h_in, p_in, m_in, eps_ref, sig_ref, E, H, S,
-        keep, drive, cx, cy, mat, cp, edge_x, edge_y,
+        keep, drive, cx, cy, mat, cp, edge_x, edge_y, row_e, row_h, row_p,
         t_ex, t_ey, t_ax, t_ay, t_c0, t_c1,
         r_ex, r_ey, r_ax, r_ay, r_c0, r_c1,
         in_sem, send_sem, recv_sem,
@@ -163,13 +163,6 @@
             (both(has_hx, has_ly), (hx, ly)),
             (both(has_lx, has_hy), (lx, hy)),
         )
-
-        barrier = pltpu.get_barrier_semaphore()
-        for present, target in links:
-
-            @pl.when(present)
-            def _():
-                pl.semaphore_signal(barrier, inc=1, device_id=target, device_id_type=MESH)
 
         mid = pl.ds(0, rows_y)
 
@@ -246,8 +239,26 @@
         rest += slot_copies(0, 0, top, 10) + across_copies(0, 15)
         kinds = [(None, pltpu.make_async_copy(m_in, mat, in_sem.at[17]))]
         later = slot_copies(1, 0, rows_x, 18) + across_copies(1, 23)
-        for copies in (rim, rest, kinds, later):
+        row_copies = [
+            (e_in.at[0, :, 0], t_ey.at[0]),
+            (e_in.at[2, :, 0], t_ey.at[1]),
+            (e_in.at[:, :, right], row_e),
+            (h_in.at[:, :, right], row_h),
+            (p_in.at[pl.ds(1, 4), :, right], row_p),
+        ]
+        line = [
+            (None, pltpu.make_async_copy(a, b, in_sem.at[25 + n]))
+            for n, (a, b) in enumerate(row_copies)
+        ]
+        for copies in (rim, line, rest, kinds, later):
             begin(copies)
+
+        barrier = pltpu.get_barrier_semaphore()
+        for present, target in links:
+
+            @pl.when(present)
+            def _():
+                pl.semaphore_signal(barrier, inc=1, device_id=target, device_id_type=MESH)
 
         zero = jnp.zeros((SUB, depth_z), jnp.float32)
         for side in (0, 1):
@@ -263,11 +274,14 @@
 
         lane = lax.broadcasted_iota(jnp.int32, (SUB, depth_z), 1)
         row = lax.broadcasted_iota(jnp.int32, (rows_y, depth_z), 0)
+        column = lax.broadcasted_iota(jnp.int32, (rows_x, depth_z), 0)
         zc = []
         for k, shift in enumerate((0.5, 0.0)):
             zc.append(profile(lane, depth_z, shift))
             for n, v in enumerate(profile(row + gy * rows_y, size_y * rows_y, shift)):
                 cy[k, n] = v
+            for n, v in enumerate(profile(column + gx * rows_x, size_x * rows_x, shift)):
+                cp[k, n] = v
 
         def clear_rest():
             for side in (0, 1):
@@ -290,13 +304,10 @@
                     E[c, i, pl.ds(rows_y, SUB), :] = zero
                     H[c, i + 1, pl.ds(0, SUB), :] = zero
 
-            column = lax.broadcasted_iota(jnp.int32, (rows_x, depth_z), 0)
             plane = lax.broadcasted_iota(jnp.int32, (rows_x, SUB, depth_z), 0)
             for k, shift in enumerate((0.5, 0.0)):
                 for n, v in enumerate(profile(plane + gx * rows_x, size_x * rows_x, shift)):
                     cx[k, n] = v
-                for n, v in enumerate(profile(column + gx * rows_x, size_x * rows_x, shift)):
-                    cp[k, n] = v
 
         def materials():
             keep_vals, drive_vals = [], []
@@ -448,14 +459,18 @@
                 late.append(packed_e(right, u))
             partial_y(late)
 
-        def partial_y(e_new):
+        def partial_y(e_new, first=False):
             for u in range(packs):
                 edge_y[pl.ds(u * SUB, SUB), :] = e_new[u][1]
             for u in range(packs):
                 i = u * SUB
                 rows = pl.ds(i, SUB)
-                old = [flat_h[across(c, i + 1, SUB + right), :] for c in range(3)]
-                aux = {n: flat_s[within(n, i, right), :] for n in (1, 2, 3, 4)}
+                if first:
+                    old = [row_h[c, rows, :] for c in range(3)]
+                    aux = {n: row_p[n - 1, rows, :] for n in (1, 2, 3, 4)}
+                else:
+                    old = [flat_h[across(c, i + 1, SUB + right), :] for c in range(3)]
+                    aux = {n: flat_s[within(n, i, right), :] for n in (1, 2, 3, 4)}
                 coef_x = [cp[0, n, rows, :] for n in range(3)]
                 side_x = (edge_y[pl.ds(i + 1, SUB), :], zero)
                 values = (e_new[u], side_x, (zero, zero), old, (), aux, coef_x)
@@ -558,15 +573,11 @@
         pl.semaphore_wait(barrier, sum(jnp.where(present, 1, 0) for present, _t in links))
         first_high, first_low, first_y = exchange(0)
         in_turn(lambda: start(first_high), lambda: start(first_low))
+        settle(line)
+        partial_y([[row_e[c, pl.ds(u * SUB, SUB), :] for c in range(3)] for u in range(packs)], True)
+        start(first_y)
         clear_rest()
         settle(rest)
-        partial_y([[flat_e[across(c, u * SUB, right), :] for c in range(3)] for u in range(packs)])
-        for u in range(packs):
-            i = u * SUB
-            rows = pl.ds(i, SUB)
-            t_ey[0, rows, :] = flat_e[across(0, i, 0), :]
-            t_ey[1, rows, :] = flat_e[across(2, i, 0), :]
-        start(first_y)
         sweep(0, count)
         settle(kinds)
         materials()
@@ -725,11 +736,14 @@
                 pltpu.VMEM((2, 3, rows_x, depth_z), f32),
                 pltpu.VMEM((3, rows_y + SUB, depth_z), f32),
                 pltpu.VMEM((rows_x + SUB, depth_z), f32),
+                pltpu.VMEM((3, rows_x, depth_z), f32),
+                pltpu.VMEM((3, rows_x, depth_z), f32),
+                pltpu.VMEM((4, rows_x, depth_z), f32),
             ]
             + [pltpu.VMEM(f, f32) for f in faces]
             + [pltpu.VMEM((2,) + f, f32) for f in faces]
             + [
-                pltpu.SemaphoreType.DMA((25,)),
+                pltpu.SemaphoreType.DMA((30,)),
                 pltpu.SemaphoreType.DMA((8,)),
                 pltpu.SemaphoreType.DMA((8, 2)),
             ],

time: 65.7 us -> 65.9 us (level)
  no operation moved by 1% of the time
where the time goes in v6:
time: 65.9 us; the launch traced here: 65.8 us
  Pallas kernels  65.1 us (99%)
    pallas_call x1, Pallas kernels, shards(): pl.pallas_call(make_kernel(size_x, size_y, rows_x, rows_y, depth_z), out_...  61.4 us
    pallas_call x1, Pallas kernels, shards(): pl.pallas_call(make_writer(size_x, size_y, rows_x, rows_y, depth_z), out_...  3.72 us

profile of v6, /device:TPU:0, one launch (start us, length us, event | category | flops | bytes accessed | tf_op | source)
XLA Modules:
  0.0 65.8 jit_solution(2006422235752131581)
XLA Ops:
  0.6 61.4 %shard_map.85 = (f32[3,33,40,128]{3,2,1,0:T(8,128)S(1)}, f32[3,33,40,128]{3,2,1,0:T(8,128)S(1)}, f32[12,32,32,128]{3,2,1,0:T(8,128)S(1)}, f32[32,32,128]{2,1,0:T...) custom-call(f32[3,32,32,128]{3,2,1,0:T(8,128)} %e_in.1, ...), custom_call_target="tpu_custom_call" | custom-call | tf_op jit(solution)/shard_map/pallas_call | solution.py:729
  62.0 3.7 %shard_map.86 = (f32[3,32,32,128]{3,2,1,0:T(8,128)}, f32[3,32,32,128]{3,2,1,0:T(8,128)}, f32[12,32,32,128]{3,2,1,0:T(8,128)}) custom-call(f32[3,33,40,128]{3,2,1,0:T(8,128)S(1)} %get-tuple-element.10.E, f32[3,33,40,128]{3,2,1,0:T(8,128)S(1)} %get-tuple-element.11.H, f32[12,32,32,128]{3,2,1,0:T(8,128)S(1)} %get-tuple-element.12.S, ...), custom_call_target="tpu_custom_call" | custom-call | tf_op jit(solution)/shard_map/pallas_call | solution.py:754
